TPU v7x, 32 devices: a whole 2x2x4 slice. The times are simulated.
32 devices in a mesh: seq: 8 (over z, y), tensor: 4 (over x, core).
Axes of the slice: x: 2, y: 2, z: 4, core: 2. Of those that a mesh axis runs over, the one named last changes fastest.
Arguments:
- fixed_point: bfloat16 [1024, 4096], P(('seq', 'tensor')), may hold values from -6 to 6
- incoming: bfloat16 [1024, 4096], P(('seq', 'tensor')), may hold values from -6 to 6
- norm_gain: float32 [4096], replicated, may hold values from 0.1 to 1.9
- query_weight: bfloat16 [4096, 4096], P(None, 'tensor'), may hold values from -0.21875 to 0.21875, as said below
- key_weight: bfloat16 [4096, 4096], P(None, 'tensor'), may hold values from -0.265625 to 0.265625, as said below
- value_weight: bfloat16 [4096, 4096], P(None, 'tensor'), may hold values from -0.09375 to 0.09375
- out_weight: bfloat16 [4096, 4096], P('tensor'), may hold values from -0.09375 to 0.09375
- layout: int32 [16, 16], replicated, may hold values 0 or 1
Outputs:
- adjoint: float32 [1024, 4096], P(('seq', 'tensor'))
- gain_grad: float32 [4096], replicated
Inputs may be any that keep to these rules, and one draw needn't show every extreme that they name: `query_weight`: entries of the columns of each head are independent; their spread may differ between heads. `key_weight`: entries are independent within a draw; columns of some heads may follow the same head's columns of query_weight. `layout`: A key block strictly before a query block is attended where the entry at row query block, column key block is 1; a block always attends itself causally; entries on or above the diagonal are not read.
All inputs are finite; a program needn't handle non-finite values.
Results may differ from a plain program's by a relative error of at most 0.03.
Values may be sent and summed in bfloat16 or wider, within the bound.
No kernel may reach another device: no remote copies, remote signals or barrier semaphores. Data moves between devices by JAX's collectives and lax.ppermute only.
A program may use at most 128 MiB of HBM per device.

v0:
```python
import functools

import jax
import jax.numpy as jnp
from jax import lax
from jax.experimental import pallas as pl
from jax.experimental.pallas import tpu as pltpu
from jax.sharding import PartitionSpec as P

HEAD_DIM = 128
BLK = 64
ITERS = 2


EPS = 1e-05
THETA = 10000.0
MASKED = -1e30


def rope_tables(positions):
    freq = THETA ** (-jnp.arange(0, HEAD_DIM, 2, dtype=jnp.float32) / HEAD_DIM)
    angle = positions.astype(jnp.float32)[:, None] * freq[None, :]
    cosine = jnp.concatenate([jnp.cos(angle), jnp.cos(angle)], axis=1)[:, None, :]
    sine = jnp.concatenate([jnp.sin(angle), jnp.sin(angle)], axis=1)[:, None, :]
    return (cosine, sine)


def rotate(values, cosine, sine):
    half = HEAD_DIM // 2
    turned = jnp.concatenate([-values[..., half:], values[..., :half]], axis=-1)
    return values * cosine + turned * sine


def rotate_back(values, cosine, sine):
    half = HEAD_DIM // 2
    weighted = values * sine
    turned = jnp.concatenate([weighted[..., half:], -weighted[..., :half]], axis=-1)
    return values * cosine + turned


def expand_blocks(chosen):
    return jnp.repeat(jnp.repeat(chosen, BLK, axis=0), BLK, axis=1)


def pair_mask(query_pos, key_pos, chosen):
    query_block = (query_pos // BLK)[:, None]
    key_block = (key_pos // BLK)[None, :]
    earlier = (key_block < query_block) & chosen
    same = (key_block == query_block) & (key_pos[None, :] <= query_pos[:, None])
    return earlier | same


def gathered_body(
    fixed_point, incoming, norm_gain, query_weight, key_weight, value_weight, out_weight, layout
):
    local_rows, model_width = fixed_point.shape
    head_width = query_weight.shape[1]
    head_count = head_width // HEAD_DIM
    seq_tokens = local_rows * lax.axis_size("tensor")
    seq_length = seq_tokens * lax.axis_size("seq")
    seq_index = lax.axis_index("seq")
    score_scale = HEAD_DIM ** (-0.5)
    contract_last = (((1,), (1,)), ((), ()))
    head_shape = (seq_tokens, head_count, HEAD_DIM)
    point = fixed_point.astype(jnp.float32)
    inv_rms = lax.rsqrt(jnp.mean(point * point, axis=1, keepdims=True) + EPS)
    scaled = point * inv_rms
    normed = (norm_gain * scaled).astype(jnp.bfloat16)
    project_piece = lax.all_gather(normed, "tensor", axis=0, tiled=True)
    projected = jnp.concatenate(
        [
            jnp.dot(project_piece, query_weight, preferred_element_type=jnp.float32),
            jnp.dot(project_piece, key_weight, preferred_element_type=jnp.float32),
            jnp.dot(project_piece, value_weight, preferred_element_type=jnp.float32),
        ],
        axis=1,
    )
    positions = seq_index * seq_tokens + jnp.arange(seq_tokens, dtype=jnp.int32)
    cosine, sine = rope_tables(positions)
    queries = rotate(projected[:, :head_width].reshape(head_shape), cosine, sine).astype(
        jnp.bfloat16
    )
    keys = rotate(
        projected[:, head_width : 2 * head_width].reshape(head_shape), cosine, sine
    ).astype(jnp.bfloat16)
    values = projected[:, 2 * head_width :].reshape(head_shape).astype(jnp.bfloat16)
    block_rows = seq_tokens // BLK
    block_count = seq_length // BLK
    first_block = seq_index * block_rows
    key_positions = jnp.arange(seq_length, dtype=jnp.int32)
    chosen_rows = (
        lax.dynamic_slice(layout, (first_block, jnp.int32(0)), (block_rows, block_count)) > 0
    )
    allowed = pair_mask(positions, key_positions, expand_blocks(chosen_rows))
    keys_all, values_all = (
        lax.all_gather(keys, "seq", axis=0, tiled=True),
        lax.all_gather(values, "seq", axis=0, tiled=True),
    )
    scores = (
        jnp.einsum("qhd,khd->hqk", queries, keys_all, preferred_element_type=jnp.float32)
        * score_scale
    )
    scores = jnp.where(allowed[None], scores, MASKED)
    log_norm = jax.nn.logsumexp(scores, axis=2, keepdims=True)
    probs = jnp.exp(scores - log_norm)
    probs_low = probs.astype(jnp.bfloat16)
    attended = jnp.einsum(
        "hqk,khd->qhd", probs_low, values_all, preferred_element_type=jnp.float32
    ).astype(jnp.bfloat16)
    cotangent = incoming.astype(jnp.float32)
    adjoint = cotangent
    gain_grad = jnp.zeros((model_width,), jnp.float32)
    for term_index in range(ITERS):
        grad_out = lax.dot_general(
            lax.all_gather(cotangent.astype(jnp.bfloat16), "tensor", axis=0, tiled=True),
            out_weight,
            contract_last,
            preferred_element_type=jnp.float32,
        )
        grad_low = grad_out.astype(jnp.bfloat16).reshape(head_shape)
        delta = jnp.sum(grad_low.astype(jnp.float32) * attended.astype(jnp.float32), axis=2)
        grad_probs = jnp.einsum(
            "qhd,khd->hqk", grad_low, values_all, preferred_element_type=jnp.float32
        )
        grad_scores = (probs * (grad_probs - delta.T[:, :, None])).astype(jnp.bfloat16)
        grad_query = (
            jnp.einsum("hqk,khd->qhd", grad_scores, keys_all, preferred_element_type=jnp.float32)
            * score_scale
        )
        key_part = (
            jnp.einsum("hqk,qhd->khd", grad_scores, queries, preferred_element_type=jnp.float32)
            * score_scale
        )
        value_part = jnp.einsum(
            "hqk,qhd->khd", probs_low, grad_low, preferred_element_type=jnp.float32
        )
        key_grads = lax.psum_scatter(
            jnp.concatenate(
                [
                    key_part.reshape(seq_tokens * lax.axis_size("seq"), head_width),
                    value_part.reshape(seq_tokens * lax.axis_size("seq"), head_width),
                ],
                axis=1,
            ).astype(jnp.bfloat16),
            "seq",
            scatter_dimension=0,
            tiled=True,
        ).astype(jnp.float32)
        grad_key = key_grads[:, :head_width].reshape(head_shape)
        grad_value = key_grads[:, head_width:].reshape(head_shape)
        query_low = (
            rotate_back(grad_query, cosine, sine)
            .astype(jnp.bfloat16)
            .reshape(seq_tokens, head_width)
        )
        key_low = (
            rotate_back(grad_key, cosine, sine).astype(jnp.bfloat16).reshape(seq_tokens, head_width)
        )
        value_low = grad_value.astype(jnp.bfloat16).reshape(seq_tokens, head_width)
        total = lax.dot_general(
            query_low, query_weight, contract_last, preferred_element_type=jnp.float32
        )
        total = total + lax.dot_general(
            key_low, key_weight, contract_last, preferred_element_type=jnp.float32
        )
        total = total + lax.dot_general(
            value_low, value_weight, contract_last, preferred_element_type=jnp.float32
        )
        grad_normed = lax.psum_scatter(
            total.astype(jnp.bfloat16), "tensor", scatter_dimension=0, tiled=True
        ).astype(jnp.float32)
        gain_term = jnp.sum(grad_normed * scaled, axis=0)
        gain_grad = gain_grad + lax.psum(gain_term, ("seq", "tensor"))
        weighted = norm_gain * grad_normed
        inner = jnp.sum(weighted * scaled, axis=1, keepdims=True)
        cotangent = inv_rms * (weighted - scaled * (inner / model_width))
        adjoint = adjoint + cotangent
    return (adjoint, gain_grad * seq_length ** (-0.5))


def xor_pairs(axis, distance):
    return [(i, i ^ distance) for i in range(lax.axis_size(axis))]


def xor_gather(block):
    blocks = {0: block}
    distance = lax.axis_size("tensor") // 2
    while distance:
        blocks.update(
            {
                j ^ distance: lax.ppermute(b, "tensor", xor_pairs("tensor", distance))
                for j, b in list(blocks.items())
            }
        )
        distance //= 2
    return [blocks[j] for j in range(len(blocks))]


def xor_reduce_scatter(blocks):
    held = dict(enumerate(blocks))
    distance = 1
    while distance < lax.axis_size("tensor"):
        keep = [j for j in held if not j & distance]
        came = [
            lax.ppermute(
                held[j ^ distance].astype(jnp.bfloat16), "tensor", xor_pairs("tensor", distance)
            )
            for j in keep
        ]
        held = {
            j: held[j].astype(jnp.float32) + c.astype(jnp.float32) for j, c in zip(keep, came)
        }
        distance *= 2
    return held[0]


def all_sum(values):
    for axis in ("tensor", "seq"):
        distance = 1
        while distance < lax.axis_size(axis):
            values = values + lax.ppermute(values, axis, xor_pairs(axis, distance))
            distance *= 2
    return values


def swap(values):
    return lax.all_to_all(values, "seq", split_axis=0, concat_axis=0, tiled=True)


def contract(a, b, da, db):
    return lax.dot_general(
        a, b, (((da,), (db,)), ((), ())), preferred_element_type=jnp.float32
    )


def in_vmem(array):
    return pltpu.with_memory_space_constraint(array, pltpu.VMEM)


def vmem_specs(count):
    return [pl.BlockSpec(memory_space=pltpu.VMEM)] * count


def join_rows(refs, joined):
    rows = refs[0].shape[0]
    for i, ref in enumerate(refs):
        joined[i * rows : (i + 1) * rows, :] = ref[...]


def load_kernel(*refs, count, pieces):
    sources, targets, semaphores = refs[:count], refs[count : 2 * count], refs[-1]
    copies = []
    for i, (source, target) in enumerate(zip(sources, targets)):
        rows = source.shape[0] // pieces
        for j in range(pieces):
            part = pl.ds(j * rows, rows)
            copies.append(
                pltpu.make_async_copy(source.at[part], target.at[part], semaphores.at[i, j])
            )
    for copy in copies:
        copy.start()
    for copy in copies:
        copy.wait()


def load(weights, pieces=4):
    size = sum(w.size for w in weights)
    return pl.pallas_call(
        functools.partial(load_kernel, count=len(weights), pieces=pieces),
        out_shape=[pltpu.VMEM(w.shape, w.dtype) for w in weights],
        in_specs=[pl.BlockSpec(memory_space=pltpu.HBM)] * len(weights),
        out_specs=vmem_specs(len(weights)),
        scratch_shapes=[pltpu.SemaphoreType.DMA((len(weights), pieces))],
        compiler_params=pltpu.CompilerParams(vmem_limit_bytes=2**20),
        cost_estimate=pl.CostEstimate(
            flops=256 * size, bytes_accessed=2 * size, transcendentals=0
        ),
    )(*(pltpu.with_memory_space_constraint(w, pltpu.HBM) for w in weights))


def pull_back_kernel(*refs, pieces):
    terms, (weight_ref, out_ref, joined) = refs[:pieces], refs[pieces:]
    join_rows(terms, joined)
    dests, _, heads, _, width = out_ref.shape
    for index in range(dests * heads):
        grad = contract(joined[...], weight_ref[index * width : (index + 1) * width, :], 1, 1)
        out_ref[index // heads, 0, index % heads] = grad.astype(jnp.bfloat16)


def pull_back(terms, weight, seq):
    rows, model = terms[0].shape
    tokens = rows * len(terms)
    heads = weight.shape[0] // HEAD_DIM
    return pl.pallas_call(
        functools.partial(pull_back_kernel, pieces=len(terms)),
        out_shape=jax.ShapeDtypeStruct((seq, 1, heads // seq, tokens, HEAD_DIM), jnp.bfloat16),
        in_specs=vmem_specs(len(terms) + 1),
        out_specs=vmem_specs(1)[0],
        scratch_shapes=[pltpu.VMEM((tokens, model), jnp.bfloat16)],
        compiler_params=pltpu.CompilerParams(vmem_limit_bytes=8 * 2**20),
        cost_estimate=pl.CostEstimate(
            flops=2 * tokens * weight.size, bytes_accessed=2 * weight.size, transcendentals=0
        ),
    )(*terms, in_vmem(weight))


def project_kernel(*refs, pieces):
    points = refs[:pieces]
    gain_ref, cos_ref, sin_ref, *weights, out_ref, inverse_ref, normed = refs[pieces:]
    rows, model = points[0].shape
    for i, ref in enumerate(points):
        point = ref[...].astype(jnp.float32)
        inverse = lax.rsqrt(jnp.mean(point * point, axis=1, keepdims=True) + EPS)
        normed[i * rows : (i + 1) * rows, :] = (gain_ref[...] * (point * inverse)).astype(
            jnp.bfloat16
        )
        inverse_ref[i * rows : (i + 1) * rows, :] = jnp.broadcast_to(
            inverse, (rows, inverse_ref.shape[1])
        )
    dests, _, heads, _, width = out_ref.shape
    group = 2 if dests * heads % 2 == 0 else 1
    for which, weight in enumerate(weights):
        for first in range(0, dests * heads, group):
            wide = contract(
                normed[...], weight[:, first * width : (first + group) * width], 1, 0
            )
            for index in range(first, first + group):
                part = wide[:, (index - first) * width : (index - first + 1) * width]
                if which < 2:
                    part = part * cos_ref[...] - pltpu.roll(part, width // 2, 1) * sin_ref[...]
                out_ref[index // heads, which, index % heads] = part.astype(jnp.bfloat16)


def project(points, gain, cosine, sine, weights, seq):
    rows, model = points[0].shape
    tokens = rows * len(points)
    heads = weights[0].shape[1] // HEAD_DIM
    return pl.pallas_call(
        functools.partial(project_kernel, pieces=len(points)),
        out_shape=[
            jax.ShapeDtypeStruct((seq, 3, heads // seq, tokens, HEAD_DIM), jnp.bfloat16),
            jax.ShapeDtypeStruct((tokens, HEAD_DIM), jnp.float32),
        ],
        in_specs=vmem_specs(len(points) + 6),
        out_specs=vmem_specs(2),
        scratch_shapes=[pltpu.VMEM((tokens, model), jnp.bfloat16)],
        compiler_params=pltpu.CompilerParams(vmem_limit_bytes=12 * 2**20),
        cost_estimate=pl.CostEstimate(
            flops=6 * tokens * weights[0].size,
            bytes_accessed=6 * weights[0].size,
            transcendentals=0,
        ),
    )(*points, gain[None], cosine, sine, *map(in_vmem, weights))


def combine_kernel(*refs, pieces):
    points = refs[:pieces]
    inverse_ref, grads_ref, *weights = refs[pieces : pieces + 5]
    blocks = refs[pieces + 5 : 2 * pieces + 5]
    gain_ref, left = refs[2 * pieces + 5 :]
    rows, model = points[0].shape
    dests, _, heads, width, _ = grads_ref.shape
    for which in range(3):
        for index in range(dests * heads):
            left[which, :, index * width : (index + 1) * width] = grads_ref[
                index // heads, which, index % heads
            ].T
    step = min(512, model)
    for start in range(0, model, step):
        columns = slice(start, start + step)
        total = contract(left[0], weights[0][columns, :], 1, 1)
        for which in (1, 2):
            total = total + contract(left[which], weights[which][columns, :], 1, 1)
        low = total.astype(jnp.bfloat16)
        gain = jnp.zeros((1, step), jnp.float32)
        for i in range(pieces):
            part = low[i * rows : (i + 1) * rows, :]
            blocks[i][:, columns] = part
            scaled = points[i][:, columns].astype(jnp.float32) * inverse_ref[
                i * rows : (i + 1) * rows, :1
            ]
            gain = gain + jnp.sum(part.astype(jnp.float32) * scaled, axis=0, keepdims=True)
        gain_ref[:, columns] = gain


def combine(points, inverse, grads, weights):
    rows, model = points[0].shape
    tokens = rows * len(points)
    *outs, gain = pl.pallas_call(
        functools.partial(combine_kernel, pieces=len(points)),
        out_shape=[jax.ShapeDtypeStruct((rows, model), jnp.bfloat16)] * len(points)
        + [jax.ShapeDtypeStruct((1, model), jnp.float32)],
        in_specs=vmem_specs(len(points) + 5),
        out_specs=vmem_specs(len(points) + 1),
        scratch_shapes=[pltpu.VMEM((3, tokens, weights[0].shape[1]), jnp.bfloat16)],
        compiler_params=pltpu.CompilerParams(vmem_limit_bytes=12 * 2**20),
        cost_estimate=pl.CostEstimate(
            flops=6 * tokens * weights[0].size,
            bytes_accessed=6 * weights[0].size,
            transcendentals=0,
        ),
    )(*points, inverse, grads, *map(in_vmem, weights))
    return outs, gain[0]


def attention_kernel(
    flip_ref, layout_ref, qkv_ref, g_ref, cos_ref, sin_ref, out_ref, key_acc, value_acc, *, step
):
    size, _, _, rows, width = g_ref.shape
    tokens = size * rows
    blocks = layout_ref.shape[0]
    flip = flip_ref[0]
    scale = width ** (-0.5)
    half = width // 2

    def turn_back(grad, start, stop):
        turned = jnp.concatenate([grad[half:], -grad[:half]], axis=0)
        cosine = jnp.concatenate([cos_ref[:, start:stop]] * 2, axis=0)
        sine = jnp.concatenate([sin_ref[:, start:stop]] * 2, axis=0)
        return (grad * cosine + turned * sine).astype(jnp.bfloat16)

    def write(which, start, stop, value):
        for block in range(start // rows, stop // rows):
            out_ref[block, which, 0] = value[:, block * rows - start : (block + 1) * rows - start]

    queries, keys, values = (qkv_ref[:, i, 0].reshape(tokens, width) for i in range(3))
    grads = g_ref[:, 0, 0].reshape(tokens, width)
    key_t, value_t = keys.T, values.T
    layout = layout_ref[...].astype(jnp.float32).astype(jnp.bfloat16)
    key_acc[...] = jnp.zeros_like(key_acc)
    value_acc[...] = jnp.zeros_like(value_acc)
    for start in range(0, tokens, step):
        seen = start + step
        query = queries[start:seen]
        grad = grads[start:seen]
        key_pos = lax.broadcasted_iota(jnp.int32, (seen, step), 0) ^ flip
        query_pos = (lax.broadcasted_iota(jnp.int32, (seen, step), 1) + start) ^ flip
        key_hot = (
            lax.broadcasted_iota(jnp.int32, (seen, blocks), 1)
            == (lax.broadcasted_iota(jnp.int32, (seen, blocks), 0) ^ flip) // BLK
        )
        query_hot = (
            lax.broadcasted_iota(jnp.int32, (blocks, step), 0)
            == ((lax.broadcasted_iota(jnp.int32, (blocks, step), 1) + start) ^ flip) // BLK
        )
        key_rows = contract(
            key_hot.astype(jnp.float32).astype(jnp.bfloat16), layout, 1, 1
        ).astype(jnp.bfloat16)
        chosen = contract(
            key_rows, query_hot.astype(jnp.float32).astype(jnp.bfloat16), 1, 0
        )
        key_block, query_block = key_pos // BLK, query_pos // BLK
        allowed = ((key_block < query_block) & (chosen > 0.5)) | (
            (key_block == query_block) & (key_pos <= query_pos)
        )
        scores = contract(keys[:seen], query, 1, 1) * scale
        scores = jnp.where(allowed, scores, MASKED)
        probs = jnp.exp(scores - jnp.max(scores, axis=0, keepdims=True))
        probs = probs / jnp.sum(probs, axis=0, keepdims=True)
        low = probs.astype(jnp.bfloat16)
        attended = contract(value_t[:, :seen], low, 1, 0).astype(jnp.bfloat16).astype(jnp.float32)
        delta = jnp.sum(attended * grad.astype(jnp.float32).T, axis=0, keepdims=True)
        grad_probs = contract(values[:seen], grad, 1, 1)
        grad_scores = (probs * (grad_probs - delta)).astype(jnp.bfloat16)
        value_acc[:seen, :] += contract(low, grad, 1, 0)
        key_acc[:seen, :] += contract(grad_scores, query, 1, 0)
        grad_query = contract(key_t[:, :seen], grad_scores, 1, 0) * scale
        write(0, start, seen, turn_back(grad_query, start, seen))
    write(1, 0, tokens, turn_back(key_acc[...].T * scale, 0, tokens))
    write(2, 0, tokens, value_acc[...].T.astype(jnp.bfloat16))


def attention_grads(flip, layout, qkv, grads, cosine, sine):
    last = grads.shape[1] - 1
    size, _, heads, rows, width = qkv.shape
    tokens = size * rows
    table = pl.BlockSpec(cosine.shape, lambda h: (0, 0))
    return pl.pallas_call(
        functools.partial(attention_kernel, step=min(max(256, rows), tokens)),
        grid=(heads,),
        out_shape=jax.ShapeDtypeStruct((size, 3, heads, width, rows), jnp.bfloat16),
        in_specs=[
            pl.BlockSpec(memory_space=pltpu.SMEM),
            pl.BlockSpec(layout.shape, lambda h: (0, 0)),
            pl.BlockSpec((size, 3, 1, rows, width), lambda h: (0, 0, h, 0, 0)),
            pl.BlockSpec((size, 1, 1, rows, width), lambda h: (0, last, h, 0, 0)),
            table,
            table,
        ],
        out_specs=pl.BlockSpec((size, 3, 1, width, rows), lambda h: (0, 0, h, 0, 0)),
        scratch_shapes=[pltpu.VMEM((tokens, width), jnp.float32)] * 2,
        compiler_params=pltpu.CompilerParams(vmem_limit_bytes=14 * 2**20),
        cost_estimate=pl.CostEstimate(
            flops=heads * 12 * tokens * tokens * width,
            bytes_accessed=heads * 16 * tokens * width,
            transcendentals=heads * tokens * tokens,
        ),
    )(flip, layout, qkv, grads, cosine, sine)


def turn_tables(positions):
    freq = THETA ** (-jnp.arange(0, HEAD_DIM, 2, dtype=jnp.float32) / HEAD_DIM)
    angle = freq[:, None] * positions.astype(jnp.float32)[None, :]
    return jnp.cos(angle), jnp.sin(angle)


def swapped_body(
    fixed_point, incoming, norm_gain, query_weight, key_weight, value_weight, out_weight, layout
):
    local_rows, model_width = fixed_point.shape
    seq = lax.axis_size("seq")
    seq_tokens = local_rows * lax.axis_size("tensor")
    seq_length = seq_tokens * seq
    flip = lax.axis_index("tensor") * local_rows
    first = lax.axis_index("seq") * seq_tokens
    *weights, flip, first = lax.optimization_barrier(
        (query_weight, key_weight, value_weight, out_weight, flip, first)
    )
    *weights, out_weight = load(weights)
    order = jnp.arange(seq_length, dtype=jnp.int32) ^ flip
    cosine, sine = turn_tables(order)
    own_cosine, own_sine = (t[:, 0] for t in rope_tables(order[:seq_tokens] + first))
    half = HEAD_DIM // 2
    own_sine = jnp.concatenate([own_sine[:, :half], -own_sine[:, half:]], axis=1)

    points = xor_gather(fixed_point)
    late_incoming, _ = lax.optimization_barrier((incoming, points[-2]))
    grad_pieces = xor_gather(late_incoming)
    sent, inverse = project(points, norm_gain, own_cosine, own_sine, weights, seq)
    sent_grads = pull_back(grad_pieces, out_weight, seq)
    sent = jnp.concatenate([sent, sent_grads], axis=1)
    sent, cosine, sine = lax.optimization_barrier((sent, cosine, sine))
    qkv = grads = swap(sent)

    inv_rms = inverse[:local_rows, :1]
    scaled = fixed_point.astype(jnp.float32) * inv_rms
    adjoint = incoming.astype(jnp.float32)
    gain_part = jnp.zeros((model_width,), jnp.float32)
    for term_index in range(ITERS):
        if term_index:
            terms = xor_gather(cotangent.astype(jnp.bfloat16))
            grads = swap(pull_back(terms, out_weight, seq))
        back = swap(attention_grads(flip[None], layout, qkv, grads, cosine, sine))
        blocks, gain_term = combine(points, inverse, back, weights)
        gain_part = gain_part + gain_term
        grad_normed = xor_reduce_scatter(blocks)
        weighted = norm_gain * grad_normed
        inner = jnp.sum(weighted * scaled, axis=1, keepdims=True)
        cotangent = inv_rms * (weighted - scaled * (inner / model_width))
        adjoint = adjoint + cotangent
    return (adjoint, all_sum(gain_part) * seq_length ** (-0.5))


def power_of_two(number):
    return number & (number - 1) == 0


def solution(mesh):
    in_specs = (
        P(("seq", "tensor"), None),
        P(("seq", "tensor"), None),
        P(),
        P(None, "tensor"),
        P(None, "tensor"),
        P(None, "tensor"),
        P("tensor", None),
        P(),
    )
    out_specs = (P(("seq", "tensor"), None), P())
    seq, tensor = mesh.shape["seq"], mesh.shape["tensor"]

    def whole(*arguments):
        local_rows = arguments[0].shape[0] // (seq * tensor)
        heads = arguments[3].shape[1] // (HEAD_DIM * tensor)
        fits = (
            heads % seq == 0
            and all(map(power_of_two, (seq, tensor, local_rows)))
            and local_rows * tensor % BLK == 0
        )
        body = swapped_body if fits else gathered_body
        return jax.shard_map(
            body, mesh=mesh, in_specs=in_specs, out_specs=out_specs, check_vma=False
        )(*arguments)

    return whole
```

profile of v0, /device:TPU:0, one launch (start us, length us, event | category | flops | bytes accessed | tf_op | source)
XLA Modules:
  0.0 190.5 jit_solution(3064686465105114020)
XLA Ops:
  0.6 3.0 %collective-permute-start.1 = (bf16[32,4096]{1,0:T(8,128)(2,1)}, bf16[32,4096]{1,0:T(8,128)(2,1)S(1)}, u32[]{:S(2)}, u32[]{:S(2)}) collective-permute-start(bf16[32,4096]{1,0:T(8,128)(2,1)} %refs_0_.7), channel_id=1, source_target_pairs={{0,2},{1,3},{2,0},{3,1},{4,6},{5,7},{6,4},{7,5},{8,10},{9,11},{10,... | collective-permute-start | bytes 786440 | tf_op jit(solution)/shard_map/ppermute | solution.py:191
  4.2 10.8 %shard_map.95 = (bf16[4096,1024]{1,0:T(8,128)(2,1)S(1)}, bf16[4096,1024]{1,0:T(8,128)(2,1)S(1)}, bf16[4096,1024]{1,0:T(8,128)(2,1)S(1)}, bf16[1024,4096]{1,0:T(8,128)(2,1)S(1)}) custom-call(bf16[4096,1024]{1,0:T(8,128)(2,1)} %refs_0_.3, bf16[4096,1024]{1,0:T(8,128)(2,1)} %refs_1_, bf16[4096,1024]{1,0:T(8,128)(2,1)} %refs_2_, bf16[1024,4096]{1,0:T(8,128)(2,1)} %refs_3_), custom_call_target="tpu_custom_call" | custom-call | flops 4294967296 | bytes 33554432 | tf_op jit(solution)/shard_map/pallas_call | solution.py:268
  15.7 1.0 multiply_sine_fusion
  16.8 6.9 %collective-permute-done.4.refs_2_ = bf16[32,4096]{1,0:T(8,128)(2,1)S(1)} collective-permute-done((bf16[32,4096]{1,0:T(8,128)(2,1)S(1)}, bf16[32,4096]{1,0:T(8,128)(2,1)S(1)}, u32[]{:S(2)}, u32[]{:S(2)}) %collective-permute-start.4) | collective-permute-done | bytes 262176 | tf_op jit(solution)/shard_map/ppermute | solution.py:191
  23.8 3.8 %shard_map.96 = (bf16[8,3,1,128,128]{4,3,2,1,0:T(8,128)(2,1)S(1)}, f32[128,128]{1,0:T(8,128)S(1)}) custom-call(bf16[32,4096]{1,0:T(8,128)(2,1)S(1)} %copy-done, bf16[32,4096]{1,0:T(8,128)(2,1)S(1)} %collective-permute-done.refs_1_, bf16[32,4096]{1,0:T(8,128)(2,1)S(1)} %collective-permute-done.1.refs_2_, bf16[32,4096]{1,0:T(8,128)(2,1)S(1)} %collective-permute-done.2.refs_3_, ...), custom_call_target="tpu_custom_call" | custom-call | flops 3221225472 | bytes 25165824 | tf_op jit(solution)/shard_map/pallas_call | solution.py:338
  27.6 2.3 %shard_map.97 = bf16[8,1,1,128,128]{4,3,2,1,0:T(8,128)(2,1)S(1)} custom-call(bf16[32,4096]{1,0:T(8,128)(2,1)S(1)} %copy-done.1, bf16[32,4096]{1,0:T(8,128)(2,1)S(1)} %collective-permute-done.3.refs_1_, bf16[32,4096]{1,0:T(8,128)(2,1)S(1)} %collective-permute-done.4.refs_2_, bf16[32,4096]{1,0:T(8,128)(2,1)S(1)} %collective-permute-done.5.refs_3_, ...), custom_call_target="tpu_custom_call" | custom-call | flops 1073741824 | bytes 8388608 | tf_op jit(solution)/shard_map/pallas_call | solution.py:294
  30.1 32.0 %all_to_all.20.qkv_ref.g_ref = bf16[8,4,1,128,128]{4,3,2,1,0:T(8,128)(2,1)S(1)} all-to-all(bf16[8,4,1,128,128]{4,3,2,1,0:T(8,128)(2,1)S(1)} %pad_maximum_fusion), channel_id=1, replica_groups=mesh['seq'=8,'tensor'=4] {'seq'}, dimensions={0} | all-to-all | bytes 2097152 | tf_op jit(solution)/shard_map/all_to_all | solution.py:227
  62.1 5.2 %shard_map.98 = bf16[8,3,1,128,128]{4,3,2,1,0:T(8,128)(2,1)S(1)} custom-call(s32[1]{0:T(128)} %bitcast.1.flip_ref, s32[16,16]{1,0:T(8,128)S(1)} %copy-done.3, bf16[8,4,1,128,128]{4,3,2,1,0:T(8,128)(2,1)S(1)} %all_to_all.20.qkv_ref.g_ref, bf16[8,4,1,128,128]{4,3,2,1,0:T(8,128)(2,1)S(1)} %all_to_all.20.qkv_ref.g_ref, ...), custom_call_target="tpu_custom_call" | custom-call | flops 1610612736 | bytes 2097152 | tf_op jit(solution)/shard_map/pallas_call | solution.py:478
  67.3 23.7 %all_to_all.21.refs_5_ = bf16[8,3,1,128,128]{4,3,2,1,0:T(8,128)(2,1)S(1)} all-to-all(bf16[8,3,1,128,128]{4,3,2,1,0:T(8,128)(2,1)S(1)} %shard_map.98), channel_id=1, replica_groups=mesh['seq'=8,'tensor'=4] {'seq'}, dimensions={0} | all-to-all | bytes 1572864 | tf_op jit(solution)/shard_map/all_to_all | solution.py:227
  91.0 8.4 %shard_map.99 = (bf16[32,4096]{1,0:T(8,128)(2,1)S(1)}, bf16[32,4096]{1,0:T(8,128)(2,1)S(1)}, bf16[32,4096]{1,0:T(8,128)(2,1)S(1)}, bf16[32,4096]{1,0:T(8,128)(2,1)S(1)}, f32[1,4096]{1,0:T(1,128)S(1)}) custom-call(bf16[32,4096]{1,0:T(8,128)(2,1)S(1)} %copy-done, bf16[32,4096]{1,0:T(8,128)(2,1)S(1)} %collective-permute-done.refs_1_, ...), custom_call_target="tpu_custom_call" | custom-call | flops 3221225472 | bytes 25165824 | tf_op jit(solution)/shard_map/pallas_call | solution.py:389
  100.0 1.0 collective-permute-done.7
  101.1 0.6 collective-permute-start.8
  101.8 7.7 %collective-permute-done.8 = bf16[32,4096]{1,0:T(8,128)(2,1)S(1)} collective-permute-done((bf16[32,4096]{1,0:T(8,128)(2,1)S(1)}, bf16[32,4096]{1,0:T(8,128)(2,1)S(1)}, u32[]{:S(2)}, u32[]{:S(2)}) %collective-permute-start.8) | collective-permute-done | bytes 262176 | tf_op jit(solution)/shard_map/ppermute | solution.py:205
  110.0 0.6 collective-permute-start.10
  110.6 7.0 %collective-permute-done.10.refs_2_ = bf16[32,4096]{1,0:T(8,128)(2,1)S(1)} collective-permute-done((bf16[32,4096]{1,0:T(8,128)(2,1)S(1)}, bf16[32,4096]{1,0:T(8,128)(2,1)S(1)}, u32[]{:S(2)}, u32[]{:S(2)}) %collective-permute-start.10) | collective-permute-done | bytes 262176 | tf_op jit(solution)/shard_map/ppermute | solution.py:191
  117.6 1.5 collective-permute-done.11.refs_3_
  119.1 2.3 %shard_map.100 = bf16[8,1,1,128,128]{4,3,2,1,0:T(8,128)(2,1)S(1)} custom-call(bf16[32,4096]{1,0:T(8,128)(2,1)S(1)} %fusion.refs_0_, bf16[32,4096]{1,0:T(8,128)(2,1)S(1)} %collective-permute-done.9.refs_1_, bf16[32,4096]{1,0:T(8,128)(2,1)S(1)} %collective-permute-done.10.refs_2_, bf16[32,4096]{1,0:T(8,128)(2,1)S(1)} %collective-permute-done.11.refs_3_, ...), custom_call_target="tpu_custom_call" | custom-call | flops 1073741824 | bytes 8388608 | tf_op jit(solution)/shard_map/pallas_call | solution.py:294
  121.5 12.7 %all_to_all.22.g_ref = bf16[8,1,1,128,128]{4,3,2,1,0:T(8,128)(2,1)S(1)} all-to-all(bf16[8,1,1,128,128]{4,3,2,1,0:T(8,128)(2,1)S(1)} %shard_map.100), channel_id=1, replica_groups=mesh['seq'=8,'tensor'=4] {'seq'}, dimensions={0} | all-to-all | bytes 524288 | tf_op jit(solution)/shard_map/all_to_all | solution.py:227
  134.1 5.1 %shard_map.101 = bf16[8,3,1,128,128]{4,3,2,1,0:T(8,128)(2,1)S(1)} custom-call(s32[1]{0:T(128)} %bitcast.1.flip_ref, s32[16,16]{1,0:T(8,128)S(1)} %copy-done.3, bf16[8,4,1,128,128]{4,3,2,1,0:T(8,128)(2,1)S(1)} %all_to_all.20.qkv_ref.g_ref, bf16[8,1,1,128,128]{4,3,2,1,0:T(8,128)(2,1)S(1)} %all_to_all.22.g_ref, f32[64,1024]{1,0:T(8,128)S(1)} %get-tuple-element.42.cos_ref, ...), custom_call_target="tpu_custom_call" | custom-call | flops 1610612736 | bytes 2097152 | tf_op jit(solution)/shard_map/pallas_call | solution.py:478
  139.3 23.2 %all_to_all.23.refs_5_ = bf16[8,3,1,128,128]{4,3,2,1,0:T(8,128)(2,1)S(1)} all-to-all(bf16[8,3,1,128,128]{4,3,2,1,0:T(8,128)(2,1)S(1)} %shard_map.101), channel_id=1, replica_groups=mesh['seq'=8,'tensor'=4] {'seq'}, dimensions={0} | all-to-all | bytes 1572864 | tf_op jit(solution)/shard_map/all_to_all | solution.py:227
  162.5 8.4 %shard_map.102 = (bf16[32,4096]{1,0:T(8,128)(2,1)S(1)}, bf16[32,4096]{1,0:T(8,128)(2,1)S(1)}, bf16[32,4096]{1,0:T(8,128)(2,1)S(1)}, bf16[32,4096]{1,0:T(8,128)(2,1)S(1)}, f32[1,4096]{1,0:T(1,128)S(1)}) custom-call(bf16[32,4096]{1,0:T(8,128)(2,1)S(1)} %copy-done, bf16[32,4096]{1,0:T(8,128)(2,1)S(1)} %collective-permute-done.refs_1_, ...), custom_call_target="tpu_custom_call" | custom-call | flops 3221225472 | bytes 25165824 | tf_op jit(solution)/shard_map/pallas_call | solution.py:389
  171.6 1.0 collective-permute-done.15
  173.1 3.2 %collective-permute-done.16 = f32[4096]{0:T(1024)S(1)} collective-permute-done((f32[4096]{0:T(1024)S(1)}, f32[4096]{0:T(1024)S(1)}, u32[]{:S(2)}, u32[]{:S(2)}) %collective-permute-start.16) | collective-permute-done | bytes 16416 | tf_op jit(solution)/shard_map/ppermute | solution.py:221
  176.3 1.5 collective-permute-start.17
  177.8 0.6 collective-permute-start.14
  178.4 1.6 collective-permute-done.17
  180.0 1.1 collective-permute-start.18
  181.1 2.6 %collective-permute-done.18 = f32[4096]{0:T(1024)S(1)} collective-permute-done((f32[4096]{0:T(1024)S(1)}, f32[4096]{0:T(1024)S(1)}, u32[]{:S(2)}, u32[]{:S(2)}) %collective-permute-start.18) | collective-permute-done | bytes 16416 | tf_op jit(solution)/shard_map/ppermute | solution.py:221
  183.8 1.1 collective-permute-start.19
  184.8 3.6 %collective-permute-done.19 = f32[4096]{0:T(1024)S(1)} collective-permute-done((f32[4096]{0:T(1024)S(1)}, f32[4096]{0:T(1024)S(1)}, u32[]{:S(2)}, u32[]{:S(2)}) %collective-permute-start.19) | collective-permute-done | bytes 16416 | tf_op jit(solution)/shard_map/ppermute | solution.py:221
  188.4 0.6 add_multiply_fusion.2
  189.3 1.2 multiply_add_fusion
  (51 shorter events, 4.2 us)
Async XLA Ops:
  0.6 14.3 %collective-permute-start.1 = (bf16[32,4096]{1,0:T(8,128)(2,1)}, bf16[32,4096]{1,0:T(8,128)(2,1)S(1)}, u32[]{:S(2)}, u32[]{:S(2)}) collective-permute-start(bf16[32,4096]{1,0:T(8,128)(2,1)} %refs_0_.7), channel_id=1, source_target_pairs={{0,2},{1,3},{2,0},{3,1},{4,6},{5,7},{6,4},{7,5},{8,10},{9,11},{10,... | collective-permute-start | bytes 786440 | tf_op jit(solution)/shard_map/ppermute | solution.py:191
  3.7 20.1 %collective-permute-start = (bf16[32,4096]{1,0:T(8,128)(2,1)}, bf16[32,4096]{1,0:T(8,128)(2,1)S(1)}, u32[]{:S(2)}, u32[]{:S(2)}) collective-permute-start(bf16[32,4096]{1,0:T(8,128)(2,1)} %refs_0_.7), channel_id=1, source_target_pairs={{0,1},{1,0},{2,3},{3,2},{4,5},{5,4},{6,7},{7,6},{8,9},{9,8},{10,11... | collective-permute-start | bytes 786440 | tf_op jit(solution)/shard_map/ppermute | solution.py:191
  4.1 10.9 %copy-start.1 = (bf16[32,4096]{1,0:T(8,128)(2,1)S(1)}, bf16[32,4096]{1,0:T(8,128)(2,1)}, u32[]{:S(2)}) copy-start(bf16[32,4096]{1,0:T(8,128)(2,1)} %refs_0_.5) | copy-start | bytes 786436
  4.1 19.6 %copy-start = (bf16[32,4096]{1,0:T(8,128)(2,1)S(1)}, bf16[32,4096]{1,0:T(8,128)(2,1)}, u32[]{:S(2)}) copy-start(bf16[32,4096]{1,0:T(8,128)(2,1)} %refs_0_.7) | copy-start | bytes 786436
  4.1 19.6 %copy-start.2 = (f32[4096]{0:T(1024)S(1)}, f32[4096]{0:T(1024)}, u32[]{:S(2)}) copy-start(f32[4096]{0:T(1024)} %param.10) | copy-start | bytes 49156
  15.0 8.8 %collective-permute-start.4 = (bf16[32,4096]{1,0:T(8,128)(2,1)S(1)}, bf16[32,4096]{1,0:T(8,128)(2,1)S(1)}, u32[]{:S(2)}, u32[]{:S(2)}) collective-permute-start(bf16[32,4096]{1,0:T(8,128)(2,1)S(1)} %copy-done.1), channel_id=1, source_target_pairs={{0,2},{1,3},{2,0},{3,1},{4,6},{5,7},{6,4},{7,5},{8,10},{9,11},{10,... | collective-permute-start | bytes 786440 | tf_op jit(solution)/shard_map/ppermute | solution.py:191
  15.2 8.6 %collective-permute-start.2 = (bf16[32,4096]{1,0:T(8,128)(2,1)S(1)}, bf16[32,4096]{1,0:T(8,128)(2,1)S(1)}, u32[]{:S(2)}, u32[]{:S(2)}) collective-permute-start(bf16[32,4096]{1,0:T(8,128)(2,1)S(1)} %collective-permute-done.1.refs_2_), channel_id=1, source_target_pairs={{0,1},{1,0},{2,3},{3,2},{4,5},{5,4},{6,7},{7,6},{8,9},{9,8},{10,11... | collective-permute-start | bytes 786440 | tf_op jit(solution)/shard_map/ppermute | solution.py:191
  16.7 10.9 %collective-permute-start.3 = (bf16[32,4096]{1,0:T(8,128)(2,1)S(1)}, bf16[32,4096]{1,0:T(8,128)(2,1)S(1)}, u32[]{:S(2)}, u32[]{:S(2)}) collective-permute-start(bf16[32,4096]{1,0:T(8,128)(2,1)S(1)} %copy-done.1), channel_id=1, source_target_pairs={{0,1},{1,0},{2,3},{3,2},{4,5},{5,4},{6,7},{7,6},{8,9},{9,8},{10,11... | collective-permute-start | bytes 786440 | tf_op jit(solution)/shard_map/ppermute | solution.py:191
  23.8 3.9 %collective-permute-start.5 = (bf16[32,4096]{1,0:T(8,128)(2,1)S(1)}, bf16[32,4096]{1,0:T(8,128)(2,1)S(1)}, u32[]{:S(2)}, u32[]{:S(2)}) collective-permute-start(bf16[32,4096]{1,0:T(8,128)(2,1)S(1)} %collective-permute-done.4.refs_2_), channel_id=1, source_target_pairs={{0,1},{1,0},{2,3},{3,2},{4,5},{5,4},{6,7},{7,6},{8,9},{9,8},{10,11... | collective-permute-start | bytes 786440 | tf_op jit(solution)/shard_map/ppermute | solution.py:191
  27.6 34.5 %copy-start.3 = (s32[16,16]{1,0:T(8,128)S(1)}, s32[16,16]{1,0:T(8,128)}, u32[]{:S(2)}) copy-start(s32[16,16]{1,0:T(8,128)} %layout_ref.3) | copy-start | bytes 3076
  99.4 1.6 collective-permute-start.7
  99.5 2.3 %collective-permute-start.6 = (bf16[32,4096]{1,0:T(8,128)(2,1)S(1)}, bf16[32,4096]{1,0:T(8,128)(2,1)S(1)}, u32[]{:S(2)}, u32[]{:S(2)}) collective-permute-start(bf16[32,4096]{1,0:T(8,128)(2,1)S(1)} %get-tuple-element.45), channel_id=1, source_target_pairs={{0,1},{1,0},{2,3},{3,2},{4,5},{5,4},{6,7},{7,6},{8,9},{9,8},{10,11... | collective-permute-start | bytes 786440 | tf_op jit(solution)/shard_map/ppermute | solution.py:205
  101.1 8.4 %collective-permute-start.8 = (bf16[32,4096]{1,0:T(8,128)(2,1)S(1)}, bf16[32,4096]{1,0:T(8,128)(2,1)S(1)}, u32[]{:S(2)}, u32[]{:S(2)}) collective-permute-start(bf16[32,4096]{1,0:T(8,128)(2,1)S(1)} %add_convert_fusion.1), channel_id=1, source_target_pairs={{0,2},{1,3},{2,0},{3,1},{4,6},{5,7},{6,4},{7,5},{8,10},{9,11},{10,... | collective-permute-start | bytes 786440 | tf_op jit(solution)/shard_map/ppermute | solution.py:205
  110.0 7.6 %collective-permute-start.10 = (bf16[32,4096]{1,0:T(8,128)(2,1)S(1)}, bf16[32,4096]{1,0:T(8,128)(2,1)S(1)}, u32[]{:S(2)}, u32[]{:S(2)}) collective-permute-start(bf16[32,4096]{1,0:T(8,128)(2,1)S(1)} %fusion.refs_0_), channel_id=1, source_target_pairs={{0,2},{1,3},{2,0},{3,1},{4,6},{5,7},{6,4},{7,5},{8,10},{9,11},{10,... | collective-permute-start | bytes 786440 | tf_op jit(solution)/shard_map/ppermute | solution.py:191
  110.6 7.0 %collective-permute-start.9 = (bf16[32,4096]{1,0:T(8,128)(2,1)S(1)}, bf16[32,4096]{1,0:T(8,128)(2,1)S(1)}, u32[]{:S(2)}, u32[]{:S(2)}) collective-permute-start(bf16[32,4096]{1,0:T(8,128)(2,1)S(1)} %fusion.refs_0_), channel_id=1, source_target_pairs={{0,1},{1,0},{2,3},{3,2},{4,5},{5,4},{6,7},{7,6},{8,9},{9,8},{10,11... | collective-permute-start | bytes 786440 | tf_op jit(solution)/shard_map/ppermute | solution.py:191
  117.6 1.5 collective-permute-start.11
  170.9 6.8 %collective-permute-start.13 = (bf16[32,4096]{1,0:T(8,128)(2,1)S(1)}, bf16[32,4096]{1,0:T(8,128)(2,1)S(1)}, u32[]{:S(2)}, u32[]{:S(2)}) collective-permute-start(bf16[32,4096]{1,0:T(8,128)(2,1)S(1)} %get-tuple-element.51), channel_id=1, source_target_pairs={{0,1},{1,0},{2,3},{3,2},{4,5},{5,4},{6,7},{7,6},{8,9},{9,8},{10,11... | collective-permute-start | bytes 786440 | tf_op jit(solution)/shard_map/ppermute | solution.py:205
  171.0 1.5 collective-permute-start.15
  172.5 3.7 %collective-permute-start.16 = (f32[4096]{0:T(1024)S(1)}, f32[4096]{0:T(1024)S(1)}, u32[]{:S(2)}, u32[]{:S(2)}) collective-permute-start(f32[4096]{0:T(1024)S(1)} %add.63), channel_id=1, source_target_pairs={{0,2},{1,3},{2,0},{3,1},{4,6},{5,7},{6,4},{7,5},{8,10},{9,11},{10,... | collective-permute-start | bytes 49160 | tf_op jit(solution)/shard_map/ppermute | solution.py:221
  173.1 16.0 %collective-permute-start.12 = (bf16[32,4096]{1,0:T(8,128)(2,1)S(1)}, bf16[32,4096]{1,0:T(8,128)(2,1)S(1)}, u32[]{:S(2)}, u32[]{:S(2)}) collective-permute-start(bf16[32,4096]{1,0:T(8,128)(2,1)S(1)} %get-tuple-element.49), channel_id=1, source_target_pairs={{0,1},{1,0},{2,3},{3,2},{4,5},{5,4},{6,7},{7,6},{8,9},{9,8},{10,11... | collective-permute-start | bytes 786440 | tf_op jit(solution)/shard_map/ppermute | solution.py:205
  176.3 3.7 %collective-permute-start.17 = (f32[4096]{0:T(1024)S(1)}, f32[4096]{0:T(1024)S(1)}, u32[]{:S(2)}, u32[]{:S(2)}) collective-permute-start(f32[4096]{0:T(1024)S(1)} %add.64), channel_id=1, source_target_pairs={{0,4},{4,0},{8,12},{12,8},{16,20},{20,16},{24,28},{28,24},{1,5},{5... | collective-permute-start | bytes 49160 | tf_op jit(solution)/shard_map/ppermute | solution.py:221
  177.8 11.2 %collective-permute-start.14 = (bf16[32,4096]{1,0:T(8,128)(2,1)S(1)}, bf16[32,4096]{1,0:T(8,128)(2,1)S(1)}, u32[]{:S(2)}, u32[]{:S(2)}) collective-permute-start(bf16[32,4096]{1,0:T(8,128)(2,1)S(1)} %add_convert_fusion), channel_id=1, source_target_pairs={{0,2},{1,3},{2,0},{3,1},{4,6},{5,7},{6,4},{7,5},{8,10},{9,11},{10,... | collective-permute-start | bytes 786440 | tf_op jit(solution)/shard_map/ppermute | solution.py:205
  180.0 3.7 %collective-permute-start.18 = (f32[4096]{0:T(1024)S(1)}, f32[4096]{0:T(1024)S(1)}, u32[]{:S(2)}, u32[]{:S(2)}) collective-permute-start(f32[4096]{0:T(1024)S(1)} %add.65), channel_id=1, source_target_pairs={{0,8},{4,12},{8,0},{12,4},{16,24},{20,28},{24,16},{28,20},{1,9},{5... | collective-permute-start | bytes 49160 | tf_op jit(solution)/shard_map/ppermute | solution.py:221
  183.8 4.6 %collective-permute-start.19 = (f32[4096]{0:T(1024)S(1)}, f32[4096]{0:T(1024)S(1)}, u32[]{:S(2)}, u32[]{:S(2)}) collective-permute-start(f32[4096]{0:T(1024)S(1)} %add.66), channel_id=1, source_target_pairs={{0,16},{4,20},{8,24},{12,28},{16,0},{20,4},{24,8},{28,12},{1,17},{... | collective-permute-start | bytes 49160 | tf_op jit(solution)/shard_map/ppermute | solution.py:221
where the time goes:
time: 191 us
  blocking collectives  91.6 us (48%)
  Pallas kernels  46.4 us (24%)
  waiting for transfers between devices  36.2 us (19%)
  starting transfers between devices  10.9 us (6%)
  other arithmetic  4.39 us (2%)
    all_to_all x4, blocking collectives, swap(): lax.all_to_all(values, 'seq', split_axis=0, concat_axis=0, tiled=True)  91.6 us
    pallas_call x2, Pallas kernels, combine(): pl.pallas_call(functools.partial(combine_kernel, pieces=len(points)), out...  16.9 us
    ppermute x9, waiting for transfers between devices, xor_gather(): lax.ppermute(b, 'tensor', xor_pairs('tensor', distance))  15.5 us
    ppermute x5, waiting for transfers between devices, all_sum(): values = values + lax.ppermute(values, axis, xor_pairs(axis, distance))  12 us
    pallas_call x1, Pallas kernels, load(): pl.pallas_call(functools.partial(load_kernel, count=len(weights), pieces=...  10.8 us
    pallas_call x2, Pallas kernels, attention_grads(): pl.pallas_call(functools.partial(attention_kernel, step=min(max(256, rows...  10.3 us
    ppermute x6, waiting for transfers between devices, xor_reduce_scatter(): lax.ppermute(held[j ^ distance].astype(jnp.bfloat16), 'tensor', xor_pairs...  8.74 us
    ppermute x5, starting transfers between devices, all_sum(): values = values + lax.ppermute(values, axis, xor_pairs(axis, distance))  4.71 us
  transfers between devices with their start and end apart: 20, of which 10 were waited for; matrix products, arithmetic and copies ran while one was open for 1% of the time, Pallas kernels for 8%

commit v1 on v0

--- a/solution.py
+++ b/solution.py
@@ -6,6 +6,7 @@
 from jax.experimental import pallas as pl
 from jax.experimental.pallas import tpu as pltpu
 from jax.sharding import PartitionSpec as P
+
 
 HEAD_DIM = 128
 BLK = 64
@@ -110,7 +111,7 @@
     cotangent = incoming.astype(jnp.float32)
     adjoint = cotangent
     gain_grad = jnp.zeros((model_width,), jnp.float32)
-    for term_index in range(ITERS):
+    for _ in range(ITERS):
         grad_out = lax.dot_general(
             lax.all_gather(cotangent.astype(jnp.bfloat16), "tensor", axis=0, tiled=True),
             out_weight,
@@ -197,29 +198,31 @@
 
 
 def xor_reduce_scatter(blocks):
-    held = dict(enumerate(blocks))
+    held = {j: [block] for j, block in enumerate(blocks)}
     distance = 1
     while distance < lax.axis_size("tensor"):
-        keep = [j for j in held if not j & distance]
-        came = [
-            lax.ppermute(
-                held[j ^ distance].astype(jnp.bfloat16), "tensor", xor_pairs("tensor", distance)
-            )
-            for j in keep
-        ]
-        held = {
-            j: held[j].astype(jnp.float32) + c.astype(jnp.float32) for j, c in zip(keep, came)
-        }
+        for j in [j for j in held if not j & distance]:
+            parts = held.pop(j ^ distance)
+            if len(parts) > 1:
+                parts = [sum(p.astype(jnp.float32) for p in parts).astype(jnp.bfloat16)]
+            held[j].append(lax.ppermute(parts[0], "tensor", xor_pairs("tensor", distance)))
         distance *= 2
     return held[0]
 
 
 def all_sum(values):
-    for axis in ("tensor", "seq"):
-        distance = 1
-        while distance < lax.axis_size(axis):
-            values = values + lax.ppermute(values, axis, xor_pairs(axis, distance))
-            distance *= 2
+    axes = ("seq", "tensor")
+    size = lax.axis_size("seq") * lax.axis_size("tensor")
+    bits = [1 << i for i in range(size.bit_length() - 1)]
+    phases = [bits[:1]] + [bits[i : i + 2] for i in range(1, len(bits), 2)][::-1]
+    for phase in phases:
+        parts = [values]
+        for flips in range(1, 1 << len(phase)):
+            distance = sum(bit for i, bit in enumerate(phase) if flips >> i & 1)
+            parts.append(lax.ppermute(values, axes, [(i, i ^ distance) for i in range(size)]))
+        while len(parts) > 1:
+            parts = [x + y for x, y in zip(parts[::2], parts[1::2])]
+        values = parts[0]
     return values
 
 
@@ -307,7 +310,7 @@
 def project_kernel(*refs, pieces):
     points = refs[:pieces]
     gain_ref, cos_ref, sin_ref, *weights, out_ref, inverse_ref, normed = refs[pieces:]
-    rows, model = points[0].shape
+    rows, _ = points[0].shape
     for i, ref in enumerate(points):
         point = ref[...].astype(jnp.float32)
         inverse = lax.rsqrt(jnp.mean(point * point, axis=1, keepdims=True) + EPS)
@@ -353,60 +356,114 @@
     )(*points, gain[None], cosine, sine, *map(in_vmem, weights))
 
 
-def combine_kernel(*refs, pieces):
-    points = refs[:pieces]
-    inverse_ref, grads_ref, *weights = refs[pieces : pieces + 5]
-    blocks = refs[pieces + 5 : 2 * pieces + 5]
-    gain_ref, left = refs[2 * pieces + 5 :]
-    rows, model = points[0].shape
-    dests, _, heads, width, _ = grads_ref.shape
-    for which in range(3):
-        for index in range(dests * heads):
-            left[which, :, index * width : (index + 1) * width] = grads_ref[
-                index // heads, which, index % heads
-            ].T
-    step = min(512, model)
-    for start in range(0, model, step):
-        columns = slice(start, start + step)
-        total = contract(left[0], weights[0][columns, :], 1, 1)
+def combine_kernel(*refs, pieces, columns, turned):
+    points, (inverse_ref, grads_ref, *weights), refs = (
+        refs[:pieces], refs[pieces : pieces + 5], refs[pieces + 5 :]
+    )
+    blocks, gain_ref = refs[:pieces], refs[pieces]
+    rows = points[0].shape[0]
+    if turned:
+        left = grads_ref
+    else:
+        left = refs[pieces + 1]
+        dests, _, heads, width, _ = grads_ref.shape
+        for which in range(3):
+            for index in range(dests * heads):
+                left[which, :, index * width : (index + 1) * width] = grads_ref[
+                    index // heads, which, index % heads
+                ].T
+    first, last = columns
+    step = min(512, last - first)
+    for start in range(first, last, step):
+        source = slice(start, start + step)
+        target = slice(start - first, start - first + step)
+        total = contract(left[0], weights[0][source, :], 1, 1)
         for which in (1, 2):
-            total = total + contract(left[which], weights[which][columns, :], 1, 1)
+            total = total + contract(left[which], weights[which][source, :], 1, 1)
         low = total.astype(jnp.bfloat16)
         gain = jnp.zeros((1, step), jnp.float32)
         for i in range(pieces):
             part = low[i * rows : (i + 1) * rows, :]
-            blocks[i][:, columns] = part
-            scaled = points[i][:, columns].astype(jnp.float32) * inverse_ref[
+            blocks[i][:, target] = part
+            scaled = points[i][:, source].astype(jnp.float32) * inverse_ref[
                 i * rows : (i + 1) * rows, :1
             ]
             gain = gain + jnp.sum(part.astype(jnp.float32) * scaled, axis=0, keepdims=True)
-        gain_ref[:, columns] = gain
-
-
-def combine(points, inverse, grads, weights):
-    rows, model = points[0].shape
-    tokens = rows * len(points)
-    *outs, gain = pl.pallas_call(
-        functools.partial(combine_kernel, pieces=len(points)),
-        out_shape=[jax.ShapeDtypeStruct((rows, model), jnp.bfloat16)] * len(points)
-        + [jax.ShapeDtypeStruct((1, model), jnp.float32)],
+        gain_ref[:, target] = gain
+
+
+def combine(points, inverse, grads, weights, columns):
+    rows = points[0].shape[0]
+    tokens, width = rows * len(points), columns[1] - columns[0]
+    turned = grads.ndim == 3
+    joined = (3, tokens, weights[0].shape[1])
+    outs = pl.pallas_call(
+        functools.partial(combine_kernel, pieces=len(points), columns=columns, turned=turned),
+        out_shape=[jax.ShapeDtypeStruct((rows, width), jnp.bfloat16)] * len(points)
+        + [jax.ShapeDtypeStruct((1, width), jnp.float32)]
+        + [pltpu.VMEM(joined, jnp.bfloat16)] * (not turned),
         in_specs=vmem_specs(len(points) + 5),
-        out_specs=vmem_specs(len(points) + 1),
-        scratch_shapes=[pltpu.VMEM((3, tokens, weights[0].shape[1]), jnp.bfloat16)],
-        compiler_params=pltpu.CompilerParams(vmem_limit_bytes=12 * 2**20),
+        out_specs=vmem_specs(len(points) + 2 - turned),
+        compiler_params=pltpu.CompilerParams(vmem_limit_bytes=8 * 2**20),
         cost_estimate=pl.CostEstimate(
-            flops=6 * tokens * weights[0].size,
-            bytes_accessed=6 * weights[0].size,
+            flops=6 * tokens * width * weights[0].shape[1],
+            bytes_accessed=6 * width * weights[0].shape[1],
             transcendentals=0,
         ),
-    )(*points, inverse, grads, *map(in_vmem, weights))
-    return outs, gain[0]
+    )(*points, inverse, in_vmem(grads) if turned else grads, *map(in_vmem, weights))
+    count = len(points)
+    return outs[:count], outs[count][0], grads if turned else outs[count + 1]
+
+
+def advance_kernel(*refs, parts):
+    sums, (point_ref, inverse_ref, gain_ref, past_ref, next_ref, total_ref) = (
+        refs[: sum(parts)], refs[sum(parts) :]
+    )
+    rows, model = point_ref.shape
+    inverse = inverse_ref[:rows, :1]
+    grads, first = [], 0
+    for count in parts:
+        group = sums[first : first + count]
+        grads.append(sum(ref[...].astype(jnp.float32) for ref in group))
+        first += count
+    edges = [0]
+    for grad in grads:
+        edges.append(edges[-1] + grad.shape[1])
+    spans = [slice(*edge) for edge in zip(edges, edges[1:])]
+    scaled = [point_ref[:, s].astype(jnp.float32) * inverse for s in spans]
+    weighted = [gain_ref[:, s] * g for s, g in zip(spans, grads)]
+    inner = sum(jnp.sum(w * x, axis=1, keepdims=True) for w, x in zip(weighted, scaled))
+    for s, w, x in zip(spans, weighted, scaled):
+        term = inverse * (w - x * (inner / model))
+        next_ref[:, s] = term.astype(jnp.bfloat16)
+        total_ref[:, s] = past_ref[:, s].astype(jnp.float32) + term
+
+
+def advance(sums, point, inverse, gain, past):
+    return pl.pallas_call(
+        functools.partial(advance_kernel, parts=[len(group) for group in sums]),
+        out_shape=[
+            jax.ShapeDtypeStruct(point.shape, jnp.bfloat16),
+            jax.ShapeDtypeStruct(point.shape, jnp.float32),
+        ],
+        in_specs=vmem_specs(sum(map(len, sums)) + 4),
+        out_specs=vmem_specs(2),
+        compiler_params=pltpu.CompilerParams(vmem_limit_bytes=8 * 2**20),
+        cost_estimate=pl.CostEstimate(
+            flops=16 * point.size, bytes_accessed=16 * point.size, transcendentals=0
+        ),
+    )(*(p for group in sums for p in group), point, inverse, gain[None], past)
 
 
 def attention_kernel(
-    flip_ref, layout_ref, qkv_ref, g_ref, cos_ref, sin_ref, out_ref, key_acc, value_acc, *, step
+    flip_ref, layout_ref, qkv_ref, g_ref, cos_ref, sin_ref, *refs, step, kept
 ):
-    size, _, _, rows, width = g_ref.shape
+    if kept:
+        probs_ref, attended_ref, out_ref, key_acc, value_acc = refs
+    else:
+        out_ref, probs_ref, attended_ref, key_acc, value_acc = refs
+    size, _, heads, rows, width = qkv_ref.shape
+    last = g_ref.shape[1] - 1
     tokens = size * rows
     blocks = layout_ref.shape[0]
     flip = flip_ref[0]
@@ -419,20 +476,7 @@
         sine = jnp.concatenate([sin_ref[:, start:stop]] * 2, axis=0)
         return (grad * cosine + turned * sine).astype(jnp.bfloat16)
 
-    def write(which, start, stop, value):
-        for block in range(start // rows, stop // rows):
-            out_ref[block, which, 0] = value[:, block * rows - start : (block + 1) * rows - start]
-
-    queries, keys, values = (qkv_ref[:, i, 0].reshape(tokens, width) for i in range(3))
-    grads = g_ref[:, 0, 0].reshape(tokens, width)
-    key_t, value_t = keys.T, values.T
-    layout = layout_ref[...].astype(jnp.float32).astype(jnp.bfloat16)
-    key_acc[...] = jnp.zeros_like(key_acc)
-    value_acc[...] = jnp.zeros_like(value_acc)
-    for start in range(0, tokens, step):
-        seen = start + step
-        query = queries[start:seen]
-        grad = grads[start:seen]
+    def probabilities(keys, query, start, seen):
         key_pos = lax.broadcasted_iota(jnp.int32, (seen, step), 0) ^ flip
         query_pos = (lax.broadcasted_iota(jnp.int32, (seen, step), 1) + start) ^ flip
         key_hot = (
@@ -443,6 +487,7 @@
             lax.broadcasted_iota(jnp.int32, (blocks, step), 0)
             == ((lax.broadcasted_iota(jnp.int32, (blocks, step), 1) + start) ^ flip) // BLK
         )
+        layout = layout_ref[...].astype(jnp.float32).astype(jnp.bfloat16)
         key_rows = contract(
             key_hot.astype(jnp.float32).astype(jnp.bfloat16), layout, 1, 1
         ).astype(jnp.bfloat16)
@@ -456,46 +501,72 @@
         scores = contract(keys[:seen], query, 1, 1) * scale
         scores = jnp.where(allowed, scores, MASKED)
         probs = jnp.exp(scores - jnp.max(scores, axis=0, keepdims=True))
-        probs = probs / jnp.sum(probs, axis=0, keepdims=True)
-        low = probs.astype(jnp.bfloat16)
-        attended = contract(value_t[:, :seen], low, 1, 0).astype(jnp.bfloat16).astype(jnp.float32)
-        delta = jnp.sum(attended * grad.astype(jnp.float32).T, axis=0, keepdims=True)
-        grad_probs = contract(values[:seen], grad, 1, 1)
-        grad_scores = (probs * (grad_probs - delta)).astype(jnp.bfloat16)
-        value_acc[:seen, :] += contract(low, grad, 1, 0)
-        key_acc[:seen, :] += contract(grad_scores, query, 1, 0)
-        grad_query = contract(key_t[:, :seen], grad_scores, 1, 0) * scale
-        write(0, start, seen, turn_back(grad_query, start, seen))
-    write(1, 0, tokens, turn_back(key_acc[...].T * scale, 0, tokens))
-    write(2, 0, tokens, value_acc[...].T.astype(jnp.bfloat16))
-
-
-def attention_grads(flip, layout, qkv, grads, cosine, sine):
-    last = grads.shape[1] - 1
+        return probs * (1.0 / jnp.sum(probs, axis=0, keepdims=True))
+
+    for head in range(heads):
+        queries, keys, values = (qkv_ref[:, i, head].reshape(tokens, width) for i in range(3))
+        grads = g_ref[:, last, head].reshape(tokens, width)
+        key_t = keys.T
+        key_acc[...] = jnp.zeros_like(key_acc)
+        value_acc[...] = jnp.zeros_like(value_acc)
+
+        def write(which, start, stop, value):
+            for block in range(start // rows, stop // rows):
+                out_ref[block, which, head] = value[
+                    :, block * rows - start : (block + 1) * rows - start
+                ]
+
+        for start in range(0, tokens, step):
+            seen = start + step
+            query, grad = queries[start:seen], grads[start:seen]
+            if kept:
+                probs = probs_ref[head, :seen, start:seen]
+            else:
+                probs = probabilities(keys, query, start, seen)
+                probs_ref[head, :seen, start:seen] = probs
+            low = probs.astype(jnp.bfloat16)
+            if kept:
+                attended = attended_ref[head, :, start:seen]
+            else:
+                attended = contract(values.T[:, :seen], low, 1, 0).astype(jnp.bfloat16)
+                attended_ref[head, :, start:seen] = attended
+            delta = jnp.sum(
+                attended.astype(jnp.float32) * grad.astype(jnp.float32).T, axis=0, keepdims=True
+            )
+            grad_probs = contract(values[:seen], grad, 1, 1)
+            grad_scores = (probs * (grad_probs - delta)).astype(jnp.bfloat16)
+            value_acc[:seen, :] += contract(low, grad, 1, 0)
+            key_acc[:seen, :] += contract(grad_scores, query, 1, 0)
+            grad_query = contract(key_t[:, :seen], grad_scores, 1, 0) * scale
+            write(0, start, seen, turn_back(grad_query, start, seen))
+        write(1, 0, tokens, turn_back(key_acc[...].T * scale, 0, tokens))
+        write(2, 0, tokens, value_acc[...].T.astype(jnp.bfloat16))
+
+
+def attention_grads(flip, layout, qkv, grads, cosine, sine, kept=()):
     size, _, heads, rows, width = qkv.shape
     tokens = size * rows
-    table = pl.BlockSpec(cosine.shape, lambda h: (0, 0))
-    return pl.pallas_call(
-        functools.partial(attention_kernel, step=min(max(256, rows), tokens)),
-        grid=(heads,),
-        out_shape=jax.ShapeDtypeStruct((size, 3, heads, width, rows), jnp.bfloat16),
-        in_specs=[
-            pl.BlockSpec(memory_space=pltpu.SMEM),
-            pl.BlockSpec(layout.shape, lambda h: (0, 0)),
-            pl.BlockSpec((size, 3, 1, rows, width), lambda h: (0, 0, h, 0, 0)),
-            pl.BlockSpec((size, 1, 1, rows, width), lambda h: (0, last, h, 0, 0)),
-            table,
-            table,
-        ],
-        out_specs=pl.BlockSpec((size, 3, 1, width, rows), lambda h: (0, 0, h, 0, 0)),
+    keep = [
+        pltpu.VMEM((heads, tokens, tokens), jnp.float32),
+        pltpu.VMEM((heads, width, tokens), jnp.bfloat16),
+    ]
+    out, *new = pl.pallas_call(
+        functools.partial(
+            attention_kernel, step=min(max(256, rows), tokens), kept=bool(kept)
+        ),
+        out_shape=[jax.ShapeDtypeStruct((size, 3, heads, width, rows), jnp.bfloat16)]
+        + keep * (not kept),
+        in_specs=[pl.BlockSpec(memory_space=pltpu.SMEM)] + vmem_specs(5 + len(kept)),
+        out_specs=vmem_specs(1 if kept else 3),
         scratch_shapes=[pltpu.VMEM((tokens, width), jnp.float32)] * 2,
-        compiler_params=pltpu.CompilerParams(vmem_limit_bytes=14 * 2**20),
+        compiler_params=pltpu.CompilerParams(vmem_limit_bytes=12 * 2**20),
         cost_estimate=pl.CostEstimate(
             flops=heads * 12 * tokens * tokens * width,
             bytes_accessed=heads * 16 * tokens * width,
-            transcendentals=heads * tokens * tokens,
+            transcendentals=0 if kept else heads * tokens * tokens,
         ),
-    )(flip, layout, qkv, grads, cosine, sine)
+    )(flip, layout, qkv, grads, cosine, sine, *map(in_vmem, kept))
+    return out, kept or tuple(new)
 
 
 def turn_tables(positions):
@@ -523,31 +594,27 @@
     half = HEAD_DIM // 2
     own_sine = jnp.concatenate([own_sine[:, :half], -own_sine[:, half:]], axis=1)
 
-    points = xor_gather(fixed_point)
-    late_incoming, _ = lax.optimization_barrier((incoming, points[-2]))
-    grad_pieces = xor_gather(late_incoming)
+    points, grad_pieces = xor_gather(fixed_point), xor_gather(incoming)
     sent, inverse = project(points, norm_gain, own_cosine, own_sine, weights, seq)
-    sent_grads = pull_back(grad_pieces, out_weight, seq)
-    sent = jnp.concatenate([sent, sent_grads], axis=1)
+    sent = jnp.concatenate([sent, pull_back(grad_pieces, out_weight, seq)], axis=1)
     sent, cosine, sine = lax.optimization_barrier((sent, cosine, sine))
     qkv = grads = swap(sent)
 
-    inv_rms = inverse[:local_rows, :1]
-    scaled = fixed_point.astype(jnp.float32) * inv_rms
-    adjoint = incoming.astype(jnp.float32)
-    gain_part = jnp.zeros((model_width,), jnp.float32)
+    cotangent = adjoint = incoming
+    middle = model_width // 2
+    gain_part, kept = jnp.zeros((model_width,), jnp.float32), ()
     for term_index in range(ITERS):
         if term_index:
-            terms = xor_gather(cotangent.astype(jnp.bfloat16))
-            grads = swap(pull_back(terms, out_weight, seq))
-        back = swap(attention_grads(flip[None], layout, qkv, grads, cosine, sine))
-        blocks, gain_term = combine(points, inverse, back, weights)
-        gain_part = gain_part + gain_term
-        grad_normed = xor_reduce_scatter(blocks)
-        weighted = norm_gain * grad_normed
-        inner = jnp.sum(weighted * scaled, axis=1, keepdims=True)
-        cotangent = inv_rms * (weighted - scaled * (inner / model_width))
-        adjoint = adjoint + cotangent
+            grads = swap(pull_back(xor_gather(cotangent), out_weight, seq))
+        back, kept = attention_grads(flip[None], layout, qkv, grads, cosine, sine, kept)
+        left = swap(back)
+        sums, gains = [], []
+        for columns in ((0, middle), (middle, model_width)):
+            blocks, gain_term, left = combine(points, inverse, left, weights, columns)
+            sums.append(xor_reduce_scatter(blocks))
+            gains.append(gain_term)
+        gain_part = gain_part + jnp.concatenate(gains)
+        cotangent, adjoint = advance(sums, fixed_point, inverse, norm_gain, adjoint)
     return (adjoint, all_sum(gain_part) * seq_length ** (-0.5))
 
 

time: 191 us -> 182 us (0.953)
  waiting for transfers between devices: 36.2 us -> 21.8 us
  starting transfers between devices: 10.9 us -> 20.2 us
  other arithmetic: 4.39 us -> 2.34 us
    ppermute x11 -> x19, starting transfers between devices: 6.54 us -> 14.4 us  [the longest x7 8.07 us: all_sum(): lax.ppermute(values, axes, [(i, i ^ distance) for i in range(size)])]
    ppermute x9, waiting for transfers between devices: 15.5 us -> 7.93 us  [xor_gather(): lax.ppermute(b, 'tensor', xor_pairs('tensor', distance))]
    ppermute x11 -> x19, waiting for transfers between devices: 20.7 us -> 13.9 us  [the longest x12 10.2 us: xor_reduce_scatter(): lax.ppermute(parts[0], 'tensor', xor_pairs('tensor', distance))]
    pallas_call x2, Pallas kernels: 10.3 us -> 7.17 us  [attention_grads(): pl.pallas_call(functools.partial(attention_kernel, step=min(max(256, rows...]
    pallas_call x2 -> x6, Pallas kernels: 16.9 us -> 18.7 us  [the longest x4 17.2 us: combine(): pl.pallas_call(functools.partial(combine_kernel, pieces=len(points), colu...]
  transfers between devices with their start and end apart: 20 -> 28, of which waited for: 10 -> 13; matrix products, arithmetic and copies ran while one was open for 1% -> 1% of each run, Pallas kernels for 8% -> 10%
where the time goes in v1:
time: 182 us
  blocking collectives  91.5 us (50%)
  Pallas kernels  45.2 us (25%)
  waiting for transfers between devices  21.8 us (12%)
  starting transfers between devices  20.2 us (11%)
  other arithmetic  2.34 us (1%)
    all_to_all x4, blocking collectives, swap(): lax.all_to_all(values, 'seq', split_axis=0, concat_axis=0, tiled=True)  91.5 us
    pallas_call x4, Pallas kernels, combine(): pl.pallas_call(functools.partial(combine_kernel, pieces=len(points), colu...  17.2 us
    pallas_call x1, Pallas kernels, load(): pl.pallas_call(functools.partial(load_kernel, count=len(weights), pieces=...  10.8 us
    ppermute x12, waiting for transfers between devices, xor_reduce_scatter(): lax.ppermute(parts[0], 'tensor', xor_pairs('tensor', distance))  10.2 us
    ppermute x7, starting transfers between devices, all_sum(): lax.ppermute(values, axes, [(i, i ^ distance) for i in range(size)])  8.07 us
    ppermute x9, waiting for transfers between devices, xor_gather(): lax.ppermute(b, 'tensor', xor_pairs('tensor', distance))  7.93 us
    pallas_call x2, Pallas kernels, attention_grads(): pl.pallas_call(functools.partial(attention_kernel, step=min(max(256, rows...  7.17 us
    ppermute x12, starting transfers between devices, xor_reduce_scatter(): lax.ppermute(parts[0], 'tensor', xor_pairs('tensor', distance))  6.38 us
  transfers between devices with their start and end apart: 28, of which 13 were waited for; matrix products, arithmetic and copies ran while one was open for 1% of the time, Pallas kernels for 10%

profile of v1, /device:TPU:0, one launch (start us, length us, event | category | flops | bytes accessed | tf_op | source)
XLA Modules:
  0.0 181.9 jit_solution(1638710526055574427)
XLA Ops:
  0.6 3.0 %collective-permute-start.4 = (bf16[32,4096]{1,0:T(8,128)(2,1)}, bf16[32,4096]{1,0:T(8,128)(2,1)S(1)}, u32[]{:S(2)}, u32[]{:S(2)}) collective-permute-start(bf16[32,4096]{1,0:T(8,128)(2,1)} %refs_9_.1), channel_id=1, source_target_pairs={{0,2},{1,3},{2,0},{3,1},{4,6},{5,7},{6,4},{7,5},{8,10},{9,11},{10,... | collective-permute-start | bytes 786440 | tf_op jit(solution)/shard_map/ppermute | solution.py:192
  4.2 10.8 %shard_map.95 = (bf16[4096,1024]{1,0:T(8,128)(2,1)S(1)}, bf16[4096,1024]{1,0:T(8,128)(2,1)S(1)}, bf16[4096,1024]{1,0:T(8,128)(2,1)S(1)}, bf16[1024,4096]{1,0:T(8,128)(2,1)S(1)}) custom-call(bf16[4096,1024]{1,0:T(8,128)(2,1)} %refs_0_.6, bf16[4096,1024]{1,0:T(8,128)(2,1)} %refs_1_, bf16[4096,1024]{1,0:T(8,128)(2,1)} %refs_2_, bf16[1024,4096]{1,0:T(8,128)(2,1)} %refs_3_), custom_call_target="tpu_custom_call" | custom-call | flops 4294967296 | bytes 33554432 | tf_op jit(solution)/shard_map/pallas_call | solution.py:271
  15.0 1.0 multiply_sine_fusion
  17.7 2.4 %shard_map.97 = bf16[8,1,1,128,128]{4,3,2,1,0:T(8,128)(2,1)S(1)} custom-call(bf16[32,4096]{1,0:T(8,128)(2,1)S(1)} %copy-done.1, bf16[32,4096]{1,0:T(8,128)(2,1)S(1)} %collective-permute-done.3.refs_1_, bf16[32,4096]{1,0:T(8,128)(2,1)S(1)} %collective-permute-done.4.refs_2_, bf16[32,4096]{1,0:T(8,128)(2,1)S(1)} %collective-permute-done.5.refs_3_, ...), custom_call_target="tpu_custom_call" | custom-call | flops 1073741824 | bytes 8388608 | tf_op jit(solution)/shard_map/pallas_call | solution.py:297
  20.1 3.8 %shard_map.96 = (bf16[8,3,1,128,128]{4,3,2,1,0:T(8,128)(2,1)S(1)}, f32[128,128]{1,0:T(8,128)S(1)}) custom-call(bf16[32,4096]{1,0:T(8,128)(2,1)S(1)} %copy-done, bf16[32,4096]{1,0:T(8,128)(2,1)S(1)} %collective-permute-done.refs_1_, bf16[32,4096]{1,0:T(8,128)(2,1)S(1)} %collective-permute-done.1.refs_2_, bf16[32,4096]{1,0:T(8,128)(2,1)S(1)} %collective-permute-done.2.refs_3_, ...), custom_call_target="tpu_custom_call" | custom-call | flops 3221225472 | bytes 25165824 | tf_op jit(solution)/shard_map/pallas_call | solution.py:341
  24.0 32.1 %all_to_all.20.qkv_ref.g_ref = bf16[8,4,1,128,128]{4,3,2,1,0:T(8,128)(2,1)S(1)} all-to-all(bf16[8,4,1,128,128]{4,3,2,1,0:T(8,128)(2,1)S(1)} %pad_maximum_fusion), channel_id=1, replica_groups=mesh['seq'=8,'tensor'=4] {'seq'}, dimensions={0} | all-to-all | bytes 2097152 | tf_op jit(solution)/shard_map/all_to_all | solution.py:230
  56.0 5.4 %shard_map.98 = (bf16[8,3,1,128,128]{4,3,2,1,0:T(8,128)(2,1)S(1)}, f32[1,1024,1024]{2,1,0:T(8,128)S(1)}, bf16[1,128,1024]{2,1,0:T(8,128)(2,1)S(1)}) custom-call(s32[1]{0:T(128)} %bitcast.1.flip_ref, s32[16,16]{1,0:T(8,128)S(1)} %copy-done.3, bf16[8,4,1,128,128]{4,3,2,1,0:T(8,128)(2,1)S(1)} %all_to_all.20.qkv_ref.g_ref, ...), custom_call_target="tpu_custom_call" | custom-call | flops 1610612736 | bytes 2097152 | tf_op jit(solution)/shard_map/pallas_call | solution.py:553
  61.5 23.6 %all_to_all.21.refs_5_ = bf16[8,3,1,128,128]{4,3,2,1,0:T(8,128)(2,1)S(1)} all-to-all(bf16[8,3,1,128,128]{4,3,2,1,0:T(8,128)(2,1)S(1)} %get-tuple-element.60), channel_id=1, replica_groups=mesh['seq'=8,'tensor'=4] {'seq'}, dimensions={0} | all-to-all | bytes 1572864 | tf_op jit(solution)/shard_map/all_to_all | solution.py:230
  85.0 4.3 %shard_map.99 = (bf16[32,2048]{1,0:T(8,128)(2,1)S(1)}, bf16[32,2048]{1,0:T(8,128)(2,1)S(1)}, bf16[32,2048]{1,0:T(8,128)(2,1)S(1)}, bf16[32,2048]{1,0:T(8,128)(2,...) custom-call(bf16[32,4096]{1,0:T(8,128)(2,1)S(1)} %copy-done, ...), custom_call_target="tpu_custom_call" | custom-call | flops 1610612736 | bytes 12582912 | tf_op jit(solution)/shard_map/pallas_call | solution.py:400
  89.9 4.3 %shard_map.100 = (bf16[32,2048]{1,0:T(8,128)(2,1)S(1)}, bf16[32,2048]{1,0:T(8,128)(2,1)S(1)}, bf16[32,2048]{1,0:T(8,128)(2,1)S(1)}, bf16[32,2048]{1,0:T(8,128)(2,1)S(1)}, f32[1,2048]{1,0:T(1,128)S(1)}) custom-call(bf16[32,4096]{1,0:T(8,128)(2,1)S(1)} %copy-done, bf16[32,4096]{1,0:T(8,128)(2,1)S(1)} %collective-permute-done.refs_1_, ...), custom_call_target="tpu_custom_call" | custom-call | flops 1610612736 | bytes 12582912 | tf_op jit(solution)/shard_map/pallas_call | solution.py:400
  94.8 1.6 collective-permute-start.8
  97.4 3.9 %collective-permute-done.8.refs_2_ = bf16[32,2048]{1,0:T(8,128)(2,1)S(1)} collective-permute-done((bf16[32,2048]{1,0:T(8,128)(2,1)S(1)}, bf16[32,2048]{1,0:T(8,128)(2,1)S(1)}, u32[]{:S(2)}, u32[]{:S(2)}) %collective-permute-start.8) | collective-permute-done | bytes 131104 | tf_op jit(solution)/shard_map/ppermute | solution.py:208
  101.3 1.9 %collective-permute-done.11.refs_5_ = bf16[32,2048]{1,0:T(8,128)(2,1)S(1)} collective-permute-done((bf16[32,2048]{1,0:T(8,128)(2,1)S(1)}, bf16[32,2048]{1,0:T(8,128)(2,1)S(1)}, u32[]{:S(2)}, u32[]{:S(2)}) %collective-permute-start.11) | collective-permute-done | bytes 131104 | tf_op jit(solution)/shard_map/ppermute | solution.py:208
  103.5 1.6 collective-permute-start.13
  105.1 5.9 %collective-permute-done.13.refs_2_ = bf16[32,4096]{1,0:T(8,128)(2,1)S(1)} collective-permute-done((bf16[32,4096]{1,0:T(8,128)(2,1)S(1)}, bf16[32,4096]{1,0:T(8,128)(2,1)S(1)}, u32[]{:S(2)}, u32[]{:S(2)}) %collective-permute-start.13) | collective-permute-done | bytes 262176 | tf_op jit(solution)/shard_map/ppermute | solution.py:192
  111.0 1.5 collective-permute-done.14.refs_3_
  112.6 2.4 %shard_map.102 = bf16[8,1,1,128,128]{4,3,2,1,0:T(8,128)(2,1)S(1)} custom-call(bf16[32,4096]{1,0:T(8,128)(2,1)S(1)} %get-tuple-element.70.refs_0_, bf16[32,4096]{1,0:T(8,128)(2,1)S(1)} %collective-permute-done.12.refs_1_, bf16[32,4096]{1,0:T(8,128)(2,1)S(1)} %collective-permute-done.13.refs_2_, bf16[32,4096]{1,0:T(8,128)(2,1)S(1)} %collective-permute-done.14.refs_3_, ...), custom_call_target="tpu_custom_call" | custom-call | flops 1073741824 | bytes 8388608 | tf_op jit(solution)/shard_map/pallas_call | solution.py:297
  114.9 12.6 %all_to_all.22.g_ref = bf16[8,1,1,128,128]{4,3,2,1,0:T(8,128)(2,1)S(1)} all-to-all(bf16[8,1,1,128,128]{4,3,2,1,0:T(8,128)(2,1)S(1)} %shard_map.102), channel_id=1, replica_groups=mesh['seq'=8,'tensor'=4] {'seq'}, dimensions={0} | all-to-all | bytes 524288 | tf_op jit(solution)/shard_map/all_to_all | solution.py:230
  127.5 1.8 shard_map.103
  129.3 23.2 %all_to_all.23.refs_5_ = bf16[8,3,1,128,128]{4,3,2,1,0:T(8,128)(2,1)S(1)} all-to-all(bf16[8,3,1,128,128]{4,3,2,1,0:T(8,128)(2,1)S(1)} %shard_map.103), channel_id=1, replica_groups=mesh['seq'=8,'tensor'=4] {'seq'}, dimensions={0} | all-to-all | bytes 1572864 | tf_op jit(solution)/shard_map/all_to_all | solution.py:230
  152.5 4.3 %shard_map.104 = (bf16[32,2048]{1,0:T(8,128)(2,1)S(1)}, bf16[32,2048]{1,0:T(8,128)(2,1)S(1)}, bf16[32,2048]{1,0:T(8,128)(2,1)S(1)}, bf16[32,2048]{1,0:T(8,128)(2...) custom-call(bf16[32,4096]{1,0:T(8,128)(2,1)S(1)} %copy-done, ...), custom_call_target="tpu_custom_call" | custom-call | flops 1610612736 | bytes 12582912 | tf_op jit(solution)/shard_map/pallas_call | solution.py:400
  156.8 4.3 %shard_map.105 = (bf16[32,2048]{1,0:T(8,128)(2,1)S(1)}, bf16[32,2048]{1,0:T(8,128)(2,1)S(1)}, bf16[32,2048]{1,0:T(8,128)(2,1)S(1)}, bf16[32,2048]{1,0:T(8,128)(2,1)S(1)}, f32[1,2048]{1,0:T(1,128)S(1)}) custom-call(bf16[32,4096]{1,0:T(8,128)(2,1)S(1)} %copy-done, bf16[32,4096]{1,0:T(8,128)(2,1)S(1)} %collective-permute-done.refs_1_, ...), custom_call_target="tpu_custom_call" | custom-call | flops 1610612736 | bytes 12582912 | tf_op jit(solution)/shard_map/pallas_call | solution.py:400
  161.2 1.2 collective-permute-done.21
  162.4 1.1 collective-permute-start.24
  163.5 1.4 collective-permute-start.23
  164.9 1.8 %collective-permute-start.22 = (f32[4096]{0:T(1024)S(1)}, f32[4096]{0:T(1024)S(1)}, u32[]{:S(2)}, u32[]{:S(2)}) collective-permute-start(f32[4096]{0:T(1024)S(1)} %add.49), channel_id=1, source_target_pairs={{0,8},{1,9},{2,10},{3,11},{4,12},{5,13},{6,14},{7,15},{8,0},{9,1},... | collective-permute-start | bytes 49160 | tf_op jit(solution)/shard_map/ppermute | solution.py:222
  168.7 2.4 %collective-permute-start.27 = (f32[4096]{0:T(1024)S(1)}, f32[4096]{0:T(1024)S(1)}, u32[]{:S(2)}, u32[]{:S(2)}) collective-permute-start(f32[4096]{0:T(1024)S(1)} %add_add_fusion), channel_id=1, source_target_pairs={{0,6},{1,7},{2,4},{3,5},{4,2},{5,3},{6,0},{7,1},{8,14},{9,15},{10,... | collective-permute-start | bytes 49160 | tf_op jit(solution)/shard_map/ppermute | solution.py:222
  172.4 1.0 collective-permute-done.27
  173.4 1.5 collective-permute-start.17
  176.3 3.0 %collective-permute-done.17.refs_2_ = bf16[32,2048]{1,0:T(8,128)(2,1)S(1)} collective-permute-done((bf16[32,2048]{1,0:T(8,128)(2,1)S(1)}, bf16[32,2048]{1,0:T(8,128)(2,1)S(1)}, u32[]{:S(2)}, u32[]{:S(2)}) %collective-permute-start.17) | collective-permute-done | bytes 131104 | tf_op jit(solution)/shard_map/ppermute | solution.py:208
  179.3 1.4 collective-permute-done.20.refs_5_
  180.7 1.2 shard_map.106
  (64 shorter events, 9.6 us)
Async XLA Ops:
  0.6 15.4 %collective-permute-start.4 = (bf16[32,4096]{1,0:T(8,128)(2,1)}, bf16[32,4096]{1,0:T(8,128)(2,1)S(1)}, u32[]{:S(2)}, u32[]{:S(2)}) collective-permute-start(bf16[32,4096]{1,0:T(8,128)(2,1)} %refs_9_.1), channel_id=1, source_target_pairs={{0,2},{1,3},{2,0},{3,1},{4,6},{5,7},{6,4},{7,5},{8,10},{9,11},{10,... | collective-permute-start | bytes 786440 | tf_op jit(solution)/shard_map/ppermute | solution.py:192
  3.7 13.5 %collective-permute-start.3 = (bf16[32,4096]{1,0:T(8,128)(2,1)}, bf16[32,4096]{1,0:T(8,128)(2,1)S(1)}, u32[]{:S(2)}, u32[]{:S(2)}) collective-permute-start(bf16[32,4096]{1,0:T(8,128)(2,1)} %refs_9_.1), channel_id=1, source_target_pairs={{0,1},{1,0},{2,3},{3,2},{4,5},{5,4},{6,7},{7,6},{8,9},{9,8},{10,11... | collective-permute-start | bytes 786440 | tf_op jit(solution)/shard_map/ppermute | solution.py:192
  3.7 12.9 %collective-permute-start.1 = (bf16[32,4096]{1,0:T(8,128)(2,1)}, bf16[32,4096]{1,0:T(8,128)(2,1)S(1)}, u32[]{:S(2)}, u32[]{:S(2)}) collective-permute-start(bf16[32,4096]{1,0:T(8,128)(2,1)} %refs_6_.3), channel_id=1, source_target_pairs={{0,2},{1,3},{2,0},{3,1},{4,6},{5,7},{6,4},{7,5},{8,10},{9,11},{10,... | collective-permute-start | bytes 786440 | tf_op jit(solution)/shard_map/ppermute | solution.py:192
  3.8 16.2 %collective-permute-start = (bf16[32,4096]{1,0:T(8,128)(2,1)}, bf16[32,4096]{1,0:T(8,128)(2,1)S(1)}, u32[]{:S(2)}, u32[]{:S(2)}) collective-permute-start(bf16[32,4096]{1,0:T(8,128)(2,1)} %refs_6_.3), channel_id=1, source_target_pairs={{0,1},{1,0},{2,3},{3,2},{4,5},{5,4},{6,7},{7,6},{8,9},{9,8},{10,11... | collective-permute-start | bytes 786440 | tf_op jit(solution)/shard_map/ppermute | solution.py:192
  4.2 13.5 %copy-start.1 = (bf16[32,4096]{1,0:T(8,128)(2,1)S(1)}, bf16[32,4096]{1,0:T(8,128)(2,1)}, u32[]{:S(2)}) copy-start(bf16[32,4096]{1,0:T(8,128)(2,1)} %refs_9_.1) | copy-start | bytes 786436
  15.0 5.0 %copy-start = (bf16[32,4096]{1,0:T(8,128)(2,1)S(1)}, bf16[32,4096]{1,0:T(8,128)(2,1)}, u32[]{:S(2)}) copy-start(bf16[32,4096]{1,0:T(8,128)(2,1)} %refs_6_.3) | copy-start | bytes 786436
  15.0 5.0 %copy-start.2 = (f32[4096]{0:T(1024)S(1)}, f32[4096]{0:T(1024)}, u32[]{:S(2)}) copy-start(f32[4096]{0:T(1024)} %param.10) | copy-start | bytes 49156
  16.1 1.6 collective-permute-start.5
  16.6 3.4 %collective-permute-start.2 = (bf16[32,4096]{1,0:T(8,128)(2,1)S(1)}, bf16[32,4096]{1,0:T(8,128)(2,1)S(1)}, u32[]{:S(2)}, u32[]{:S(2)}) collective-permute-start(bf16[32,4096]{1,0:T(8,128)(2,1)S(1)} %collective-permute-done.1.refs_2_), channel_id=1, source_target_pairs={{0,1},{1,0},{2,3},{3,2},{4,5},{5,4},{6,7},{7,6},{8,9},{9,8},{10,11... | collective-permute-start | bytes 786440 | tf_op jit(solution)/shard_map/ppermute | solution.py:192
  20.1 36.0 %copy-start.3 = (s32[16,16]{1,0:T(8,128)S(1)}, s32[16,16]{1,0:T(8,128)}, u32[]{:S(2)}) copy-start(s32[16,16]{1,0:T(8,128)} %layout_ref.3) | copy-start | bytes 3076
  89.4 8.1 %collective-permute-start.6 = (bf16[32,2048]{1,0:T(8,128)(2,1)S(1)}, bf16[32,2048]{1,0:T(8,128)(2,1)S(1)}, u32[]{:S(2)}, u32[]{:S(2)}) collective-permute-start(bf16[32,2048]{1,0:T(8,128)(2,1)S(1)} %get-tuple-element.62), channel_id=1, source_target_pairs={{0,1},{1,0},{2,3},{3,2},{4,5},{5,4},{6,7},{7,6},{8,9},{9,8},{10,11... | collective-permute-start | bytes 393224 | tf_op jit(solution)/shard_map/ppermute | solution.py:208
  89.4 5.4 %collective-permute-start.7 = (bf16[32,2048]{1,0:T(8,128)(2,1)S(1)}, bf16[32,2048]{1,0:T(8,128)(2,1)S(1)}, u32[]{:S(2)}, u32[]{:S(2)}) collective-permute-start(bf16[32,2048]{1,0:T(8,128)(2,1)S(1)} %get-tuple-element.64), channel_id=1, source_target_pairs={{0,1},{1,0},{2,3},{3,2},{4,5},{5,4},{6,7},{7,6},{8,9},{9,8},{10,11... | collective-permute-start | bytes 393224 | tf_op jit(solution)/shard_map/ppermute | solution.py:208
  94.2 3.2 %collective-permute-start.9 = (bf16[32,2048]{1,0:T(8,128)(2,1)S(1)}, bf16[32,2048]{1,0:T(8,128)(2,1)S(1)}, u32[]{:S(2)}, u32[]{:S(2)}) collective-permute-start(bf16[32,2048]{1,0:T(8,128)(2,1)S(1)} %get-tuple-element.67), channel_id=1, source_target_pairs={{0,1},{1,0},{2,3},{3,2},{4,5},{5,4},{6,7},{7,6},{8,9},{9,8},{10,11... | collective-permute-start | bytes 393224 | tf_op jit(solution)/shard_map/ppermute | solution.py:208
  94.4 2.0 %collective-permute-start.10 = (bf16[32,2048]{1,0:T(8,128)(2,1)S(1)}, bf16[32,2048]{1,0:T(8,128)(2,1)S(1)}, u32[]{:S(2)}, u32[]{:S(2)}) collective-permute-start(bf16[32,2048]{1,0:T(8,128)(2,1)S(1)} %get-tuple-element.69), channel_id=1, source_target_pairs={{0,1},{1,0},{2,3},{3,2},{4,5},{5,4},{6,7},{7,6},{8,9},{9,8},{10,11... | collective-permute-start | bytes 393224 | tf_op jit(solution)/shard_map/ppermute | solution.py:208
  94.8 6.4 %collective-permute-start.8 = (bf16[32,2048]{1,0:T(8,128)(2,1)S(1)}, bf16[32,2048]{1,0:T(8,128)(2,1)S(1)}, u32[]{:S(2)}, u32[]{:S(2)}) collective-permute-start(bf16[32,2048]{1,0:T(8,128)(2,1)S(1)} %add_convert_fusion.3), channel_id=1, source_target_pairs={{0,2},{1,3},{2,0},{3,1},{4,6},{5,7},{6,4},{7,5},{8,10},{9,11},{10,... | collective-permute-start | bytes 393224 | tf_op jit(solution)/shard_map/ppermute | solution.py:208
  96.4 6.8 %collective-permute-start.11 = (bf16[32,2048]{1,0:T(8,128)(2,1)S(1)}, bf16[32,2048]{1,0:T(8,128)(2,1)S(1)}, u32[]{:S(2)}, u32[]{:S(2)}) collective-permute-start(bf16[32,2048]{1,0:T(8,128)(2,1)S(1)} %add_convert_fusion.2), channel_id=1, source_target_pairs={{0,2},{1,3},{2,0},{3,1},{4,6},{5,7},{6,4},{7,5},{8,10},{9,11},{10,... | collective-permute-start | bytes 393224 | tf_op jit(solution)/shard_map/ppermute | solution.py:208
  103.5 7.5 %collective-permute-start.13 = (bf16[32,4096]{1,0:T(8,128)(2,1)S(1)}, bf16[32,4096]{1,0:T(8,128)(2,1)S(1)}, u32[]{:S(2)}, u32[]{:S(2)}) collective-permute-start(bf16[32,4096]{1,0:T(8,128)(2,1)S(1)} %get-tuple-element.70.refs_0_), channel_id=1, source_target_pairs={{0,2},{1,3},{2,0},{3,1},{4,6},{5,7},{6,4},{7,5},{8,10},{9,11},{10,... | collective-permute-start | bytes 786440 | tf_op jit(solution)/shard_map/ppermute | solution.py:192
  105.1 5.9 %collective-permute-start.12 = (bf16[32,4096]{1,0:T(8,128)(2,1)S(1)}, bf16[32,4096]{1,0:T(8,128)(2,1)S(1)}, u32[]{:S(2)}, u32[]{:S(2)}) collective-permute-start(bf16[32,4096]{1,0:T(8,128)(2,1)S(1)} %get-tuple-element.70.refs_0_), channel_id=1, source_target_pairs={{0,1},{1,0},{2,3},{3,2},{4,5},{5,4},{6,7},{7,6},{8,9},{9,8},{10,11... | collective-permute-start | bytes 786440 | tf_op jit(solution)/shard_map/ppermute | solution.py:192
  111.0 1.5 collective-permute-start.14
  161.1 1.2 collective-permute-start.21
  162.4 5.5 %collective-permute-start.24 = (f32[4096]{0:T(1024)S(1)}, f32[4096]{0:T(1024)S(1)}, u32[]{:S(2)}, u32[]{:S(2)}) collective-permute-start(f32[4096]{0:T(1024)S(1)} %add.49), channel_id=1, source_target_pairs={{0,24},{1,25},{2,26},{3,27},{4,28},{5,29},{6,30},{7,31},{8,16},{9,... | collective-permute-start | bytes 49160 | tf_op jit(solution)/shard_map/ppermute | solution.py:222
  163.5 4.8 %collective-permute-start.23 = (f32[4096]{0:T(1024)S(1)}, f32[4096]{0:T(1024)S(1)}, u32[]{:S(2)}, u32[]{:S(2)}) collective-permute-start(f32[4096]{0:T(1024)S(1)} %add.49), channel_id=1, source_target_pairs={{0,16},{1,17},{2,18},{3,19},{4,20},{5,21},{6,22},{7,23},{8,24},{9,... | collective-permute-start | bytes 49160 | tf_op jit(solution)/shard_map/ppermute | solution.py:222
  164.9 3.7 %collective-permute-start.22 = (f32[4096]{0:T(1024)S(1)}, f32[4096]{0:T(1024)S(1)}, u32[]{:S(2)}, u32[]{:S(2)}) collective-permute-start(f32[4096]{0:T(1024)S(1)} %add.49), channel_id=1, source_target_pairs={{0,8},{1,9},{2,10},{3,11},{4,12},{5,13},{6,14},{7,15},{8,0},{9,1},... | collective-permute-start | bytes 49160 | tf_op jit(solution)/shard_map/ppermute | solution.py:222
  166.7 9.6 %collective-permute-start.15 = (bf16[32,2048]{1,0:T(8,128)(2,1)S(1)}, bf16[32,2048]{1,0:T(8,128)(2,1)S(1)}, u32[]{:S(2)}, u32[]{:S(2)}) collective-permute-start(bf16[32,2048]{1,0:T(8,128)(2,1)S(1)} %get-tuple-element.74), channel_id=1, source_target_pairs={{0,1},{1,0},{2,3},{3,2},{4,5},{5,4},{6,7},{7,6},{8,9},{9,8},{10,11... | collective-permute-start | bytes 393224 | tf_op jit(solution)/shard_map/ppermute | solution.py:208
  166.7 4.3 %collective-permute-start.16 = (bf16[32,2048]{1,0:T(8,128)(2,1)S(1)}, bf16[32,2048]{1,0:T(8,128)(2,1)S(1)}, u32[]{:S(2)}, u32[]{:S(2)}) collective-permute-start(bf16[32,2048]{1,0:T(8,128)(2,1)S(1)} %get-tuple-element.76), channel_id=1, source_target_pairs={{0,1},{1,0},{2,3},{3,2},{4,5},{5,4},{6,7},{7,6},{8,9},{9,8},{10,11... | collective-permute-start | bytes 393224 | tf_op jit(solution)/shard_map/ppermute | solution.py:208
  167.9 8.4 %collective-permute-start.18 = (bf16[32,2048]{1,0:T(8,128)(2,1)S(1)}, bf16[32,2048]{1,0:T(8,128)(2,1)S(1)}, u32[]{:S(2)}, u32[]{:S(2)}) collective-permute-start(bf16[32,2048]{1,0:T(8,128)(2,1)S(1)} %get-tuple-element.79), channel_id=1, source_target_pairs={{0,1},{1,0},{2,3},{3,2},{4,5},{5,4},{6,7},{7,6},{8,9},{9,8},{10,11... | collective-permute-start | bytes 393224 | tf_op jit(solution)/shard_map/ppermute | solution.py:208
  168.2 3.5 %collective-permute-start.19 = (bf16[32,2048]{1,0:T(8,128)(2,1)S(1)}, bf16[32,2048]{1,0:T(8,128)(2,1)S(1)}, u32[]{:S(2)}, u32[]{:S(2)}) collective-permute-start(bf16[32,2048]{1,0:T(8,128)(2,1)S(1)} %get-tuple-element.81), channel_id=1, source_target_pairs={{0,1},{1,0},{2,3},{3,2},{4,5},{5,4},{6,7},{7,6},{8,9},{9,8},{10,11... | collective-permute-start | bytes 393224 | tf_op jit(solution)/shard_map/ppermute | solution.py:208
  168.7 4.7 %collective-permute-start.27 = (f32[4096]{0:T(1024)S(1)}, f32[4096]{0:T(1024)S(1)}, u32[]{:S(2)}, u32[]{:S(2)}) collective-permute-start(f32[4096]{0:T(1024)S(1)} %add_add_fusion), channel_id=1, source_target_pairs={{0,6},{1,7},{2,4},{3,5},{4,2},{5,3},{6,0},{7,1},{8,14},{9,15},{10,... | collective-permute-start | bytes 49160 | tf_op jit(solution)/shard_map/ppermute | solution.py:222
  171.0 3.8 %collective-permute-start.26 = (f32[4096]{0:T(1024)S(1)}, f32[4096]{0:T(1024)S(1)}, u32[]{:S(2)}, u32[]{:S(2)}) collective-permute-start(f32[4096]{0:T(1024)S(1)} %add_add_fusion), channel_id=1, source_target_pairs={{0,4},{1,5},{2,6},{3,7},{4,0},{5,1},{6,2},{7,3},{8,12},{9,13},{10,... | collective-permute-start | bytes 49160 | tf_op jit(solution)/shard_map/ppermute | solution.py:222
  171.7 4.0 %collective-permute-start.25 = (f32[4096]{0:T(1024)S(1)}, f32[4096]{0:T(1024)S(1)}, u32[]{:S(2)}, u32[]{:S(2)}) collective-permute-start(f32[4096]{0:T(1024)S(1)} %add_add_fusion), channel_id=1, source_target_pairs={{0,2},{1,3},{2,0},{3,1},{4,6},{5,7},{6,4},{7,5},{8,10},{9,11},{10,... | collective-permute-start | bytes 49160 | tf_op jit(solution)/shard_map/ppermute | solution.py:222
  173.4 5.9 %collective-permute-start.17 = (bf16[32,2048]{1,0:T(8,128)(2,1)S(1)}, bf16[32,2048]{1,0:T(8,128)(2,1)S(1)}, u32[]{:S(2)}, u32[]{:S(2)}) collective-permute-start(bf16[32,2048]{1,0:T(8,128)(2,1)S(1)} %add_convert_fusion.1), channel_id=1, source_target_pairs={{0,2},{1,3},{2,0},{3,1},{4,6},{5,7},{6,4},{7,5},{8,10},{9,11},{10,... | collective-permute-start | bytes 393224 | tf_op jit(solution)/shard_map/ppermute | solution.py:208
  174.9 5.8 %collective-permute-start.20 = (bf16[32,2048]{1,0:T(8,128)(2,1)S(1)}, bf16[32,2048]{1,0:T(8,128)(2,1)S(1)}, u32[]{:S(2)}, u32[]{:S(2)}) collective-permute-start(bf16[32,2048]{1,0:T(8,128)(2,1)S(1)} %add_convert_fusion), channel_id=1, source_target_pairs={{0,2},{1,3},{2,0},{3,1},{4,6},{5,7},{6,4},{7,5},{8,10},{9,11},{10,... | collective-permute-start | bytes 393224 | tf_op jit(solution)/shard_map/ppermute | solution.py:208

commit v2 on v1

--- a/solution.py
+++ b/solution.py
@@ -250,35 +250,46 @@
         joined[i * rows : (i + 1) * rows, :] = ref[...]
 
 
-def load_kernel(*refs, count, pieces):
-    sources, targets, semaphores = refs[:count], refs[count : 2 * count], refs[-1]
+PIECES = 4
+
+
+def in_hbm(array):
+    return pltpu.with_memory_space_constraint(array, pltpu.HBM)
+
+
+def copies_of(source, target, semaphores):
+    rows = source.shape[0] // PIECES
+    return [
+        pltpu.make_async_copy(
+            source.at[pl.ds(j * rows, rows)], target.at[pl.ds(j * rows, rows)], semaphores.at[j]
+        )
+        for j in range(PIECES)
+    ]
+
+
+def load_kernel(*refs, count):
     copies = []
-    for i, (source, target) in enumerate(zip(sources, targets)):
-        rows = source.shape[0] // pieces
-        for j in range(pieces):
-            part = pl.ds(j * rows, rows)
-            copies.append(
-                pltpu.make_async_copy(source.at[part], target.at[part], semaphores.at[i, j])
-            )
+    for i in range(count):
+        copies += copies_of(refs[i], refs[count + i], refs[-1].at[i])
     for copy in copies:
         copy.start()
     for copy in copies:
         copy.wait()
 
 
-def load(weights, pieces=4):
+def load(weights):
     size = sum(w.size for w in weights)
     return pl.pallas_call(
-        functools.partial(load_kernel, count=len(weights), pieces=pieces),
+        functools.partial(load_kernel, count=len(weights)),
         out_shape=[pltpu.VMEM(w.shape, w.dtype) for w in weights],
         in_specs=[pl.BlockSpec(memory_space=pltpu.HBM)] * len(weights),
         out_specs=vmem_specs(len(weights)),
-        scratch_shapes=[pltpu.SemaphoreType.DMA((len(weights), pieces))],
+        scratch_shapes=[pltpu.SemaphoreType.DMA((len(weights), PIECES))],
         compiler_params=pltpu.CompilerParams(vmem_limit_bytes=2**20),
         cost_estimate=pl.CostEstimate(
             flops=256 * size, bytes_accessed=2 * size, transcendentals=0
         ),
-    )(*(pltpu.with_memory_space_constraint(w, pltpu.HBM) for w in weights))
+    )(*map(in_hbm, weights))
 
 
 def pull_back_kernel(*refs, pieces):
@@ -309,8 +320,12 @@
 
 def project_kernel(*refs, pieces):
     points = refs[:pieces]
-    gain_ref, cos_ref, sin_ref, *weights, out_ref, inverse_ref, normed = refs[pieces:]
+    gain_ref, cos_ref, sin_ref, *weights, far_ref = refs[pieces : pieces + 6]
+    out_ref, inverse_ref, last_ref, normed, semaphores = refs[pieces + 6 :]
     rows, _ = points[0].shape
+    copies = copies_of(far_ref, last_ref, semaphores)
+    for copy in copies:
+        copy.start()
     for i, ref in enumerate(points):
         point = ref[...].astype(jnp.float32)
         inverse = lax.rsqrt(jnp.mean(point * point, axis=1, keepdims=True) + EPS)
@@ -322,7 +337,10 @@
         )
     dests, _, heads, _, width = out_ref.shape
     group = 2 if dests * heads % 2 == 0 else 1
-    for which, weight in enumerate(weights):
+    for which, weight in enumerate((*weights, last_ref)):
+        if which == 2:
+            for copy in copies:
+                copy.wait()
         for first in range(0, dests * heads, group):
             wide = contract(
                 normed[...], weight[:, first * width : (first + group) * width], 1, 0
@@ -335,6 +353,7 @@
 
 
 def project(points, gain, cosine, sine, weights, seq):
+    *weights, last = weights
     rows, model = points[0].shape
     tokens = rows * len(points)
     heads = weights[0].shape[1] // HEAD_DIM
@@ -343,44 +362,45 @@
         out_shape=[
             jax.ShapeDtypeStruct((seq, 3, heads // seq, tokens, HEAD_DIM), jnp.bfloat16),
             jax.ShapeDtypeStruct((tokens, HEAD_DIM), jnp.float32),
+            pltpu.VMEM(last.shape, last.dtype),
         ],
-        in_specs=vmem_specs(len(points) + 6),
-        out_specs=vmem_specs(2),
-        scratch_shapes=[pltpu.VMEM((tokens, model), jnp.bfloat16)],
+        in_specs=vmem_specs(len(points) + 5) + [pl.BlockSpec(memory_space=pltpu.HBM)],
+        out_specs=vmem_specs(3),
+        scratch_shapes=[
+            pltpu.VMEM((tokens, model), jnp.bfloat16),
+            pltpu.SemaphoreType.DMA((PIECES,)),
+        ],
         compiler_params=pltpu.CompilerParams(vmem_limit_bytes=12 * 2**20),
         cost_estimate=pl.CostEstimate(
             flops=6 * tokens * weights[0].size,
             bytes_accessed=6 * weights[0].size,
             transcendentals=0,
         ),
-    )(*points, gain[None], cosine, sine, *map(in_vmem, weights))
-
-
-def combine_kernel(*refs, pieces, columns, turned):
+    )(*points, gain[None], cosine, sine, *map(in_vmem, weights), in_hbm(last))
+
+
+def combine_kernel(*refs, pieces, columns):
     points, (inverse_ref, grads_ref, *weights), refs = (
         refs[:pieces], refs[pieces : pieces + 5], refs[pieces + 5 :]
     )
     blocks, gain_ref = refs[:pieces], refs[pieces]
     rows = points[0].shape[0]
-    if turned:
-        left = grads_ref
-    else:
-        left = refs[pieces + 1]
-        dests, _, heads, width, _ = grads_ref.shape
-        for which in range(3):
-            for index in range(dests * heads):
-                left[which, :, index * width : (index + 1) * width] = grads_ref[
-                    index // heads, which, index % heads
-                ].T
+    dests, _, heads, width, tokens = grads_ref.shape
     first, last = columns
     step = min(512, last - first)
     for start in range(first, last, step):
         source = slice(start, start + step)
         target = slice(start - first, start - first + step)
-        total = contract(left[0], weights[0][source, :], 1, 1)
-        for which in (1, 2):
-            total = total + contract(left[which], weights[which][source, :], 1, 1)
-        low = total.astype(jnp.bfloat16)
+        total = sum(
+            contract(
+                weights[which][source, :],
+                grads_ref[:, which].reshape(dests * heads * width, tokens),
+                1,
+                0,
+            )
+            for which in range(3)
+        )
+        low = total.T.astype(jnp.bfloat16)
         gain = jnp.zeros((1, step), jnp.float32)
         for i in range(pieces):
             part = low[i * rows : (i + 1) * rows, :]
@@ -395,24 +415,20 @@
 def combine(points, inverse, grads, weights, columns):
     rows = points[0].shape[0]
     tokens, width = rows * len(points), columns[1] - columns[0]
-    turned = grads.ndim == 3
-    joined = (3, tokens, weights[0].shape[1])
-    outs = pl.pallas_call(
-        functools.partial(combine_kernel, pieces=len(points), columns=columns, turned=turned),
+    *outs, gain = pl.pallas_call(
+        functools.partial(combine_kernel, pieces=len(points), columns=columns),
         out_shape=[jax.ShapeDtypeStruct((rows, width), jnp.bfloat16)] * len(points)
-        + [jax.ShapeDtypeStruct((1, width), jnp.float32)]
-        + [pltpu.VMEM(joined, jnp.bfloat16)] * (not turned),
+        + [jax.ShapeDtypeStruct((1, width), jnp.float32)],
         in_specs=vmem_specs(len(points) + 5),
-        out_specs=vmem_specs(len(points) + 2 - turned),
+        out_specs=vmem_specs(len(points) + 1),
         compiler_params=pltpu.CompilerParams(vmem_limit_bytes=8 * 2**20),
         cost_estimate=pl.CostEstimate(
             flops=6 * tokens * width * weights[0].shape[1],
             bytes_accessed=6 * width * weights[0].shape[1],
             transcendentals=0,
         ),
-    )(*points, inverse, in_vmem(grads) if turned else grads, *map(in_vmem, weights))
-    count = len(points)
-    return outs[:count], outs[count][0], grads if turned else outs[count + 1]
+    )(*points, inverse, in_vmem(grads), *map(in_vmem, weights))
+    return outs, gain[0]
 
 
 def advance_kernel(*refs, parts):
@@ -585,7 +601,7 @@
     flip = lax.axis_index("tensor") * local_rows
     first = lax.axis_index("seq") * seq_tokens
     *weights, flip, first = lax.optimization_barrier(
-        (query_weight, key_weight, value_weight, out_weight, flip, first)
+        (query_weight, key_weight, out_weight, flip, first)
     )
     *weights, out_weight = load(weights)
     order = jnp.arange(seq_length, dtype=jnp.int32) ^ flip
@@ -595,7 +611,10 @@
     own_sine = jnp.concatenate([own_sine[:, :half], -own_sine[:, half:]], axis=1)
 
     points, grad_pieces = xor_gather(fixed_point), xor_gather(incoming)
-    sent, inverse = project(points, norm_gain, own_cosine, own_sine, weights, seq)
+    sent, inverse, value_weight = project(
+        points, norm_gain, own_cosine, own_sine, (*weights, value_weight), seq
+    )
+    weights = (*weights, value_weight)
     sent = jnp.concatenate([sent, pull_back(grad_pieces, out_weight, seq)], axis=1)
     sent, cosine, sine = lax.optimization_barrier((sent, cosine, sine))
     qkv = grads = swap(sent)
@@ -610,7 +629,7 @@
         left = swap(back)
         sums, gains = [], []
         for columns in ((0, middle), (middle, model_width)):
-            blocks, gain_term, left = combine(points, inverse, left, weights, columns)
+            blocks, gain_term = combine(points, inverse, left, weights, columns)
             sums.append(xor_reduce_scatter(blocks))
             gains.append(gain_term)
         gain_part = gain_part + jnp.concatenate(gains)

time: 182 us -> 179 us (0.984)
  Pallas kernels: 45.2 us -> 41 us
    pallas_call x4, Pallas kernels: 17.2 us -> 14.3 us  [combine(): pl.pallas_call(functools.partial(combine_kernel, pieces=len(points), colu...]
    pallas_call x1, Pallas kernels: 10.8 us -> 8.38 us  [load(): pl.pallas_call(functools.partial(load_kernel, count=len(weights)), out_sh...]
  transfers between devices with their start and end apart: 28 -> 28, of which waited for: 13 -> 13; matrix products, arithmetic and copies ran while one was open for 1% -> 1% of each run, Pallas kernels for 10% -> 8%
where the time goes in v2:
time: 179 us
  blocking collectives  91.9 us (51%)
  Pallas kernels  41 us (23%)
  waiting for transfers between devices  23 us (13%)
  starting transfers between devices  19.8 us (11%)
  other arithmetic  2.34 us (1%)
    all_to_all x4, blocking collectives, swap(): lax.all_to_all(values, 'seq', split_axis=0, concat_axis=0, tiled=True)  91.9 us
    pallas_call x4, Pallas kernels, combine(): pl.pallas_call(functools.partial(combine_kernel, pieces=len(points), colu...  14.3 us
    ppermute x12, waiting for transfers between devices, xor_reduce_scatter(): lax.ppermute(parts[0], 'tensor', xor_pairs('tensor', distance))  10.2 us
    ppermute x9, waiting for transfers between devices, xor_gather(): lax.ppermute(b, 'tensor', xor_pairs('tensor', distance))  9.11 us
    pallas_call x1, Pallas kernels, load(): pl.pallas_call(functools.partial(load_kernel, count=len(weights)), out_sh...  8.38 us
    ppermute x7, starting transfers between devices, all_sum(): lax.ppermute(values, axes, [(i, i ^ distance) for i in range(size)])  8.07 us
    pallas_call x2, Pallas kernels, attention_grads(): pl.pallas_call(functools.partial(attention_kernel, step=min(max(256, rows...  7.18 us
    ppermute x12, starting transfers between devices, xor_reduce_scatter(): lax.ppermute(parts[0], 'tensor', xor_pairs('tensor', distance))  6.35 us
  transfers between devices with their start and end apart: 28, of which 13 were waited for; matrix products, arithmetic and copies ran while one was open for 1% of the time, Pallas kernels for 8%

profile of v2, /device:TPU:0, one launch (start us, length us, event | category | flops | bytes accessed | tf_op | source)
XLA Modules:
  0.0 178.9 jit_solution(10508456198903334180)
XLA Ops:
  0.6 3.0 %collective-permute-start.4 = (bf16[32,4096]{1,0:T(8,128)(2,1)}, bf16[32,4096]{1,0:T(8,128)(2,1)S(1)}, u32[]{:S(2)}, u32[]{:S(2)}) collective-permute-start(bf16[32,4096]{1,0:T(8,128)(2,1)} %refs_9_.3), channel_id=1, source_target_pairs={{0,2},{1,3},{2,0},{3,1},{4,6},{5,7},{6,4},{7,5},{8,10},{9,11},{10,... | collective-permute-start | bytes 786440 | tf_op jit(solution)/shard_map/ppermute | solution.py:192
  4.2 8.4 %shard_map.95 = (bf16[4096,1024]{1,0:T(8,128)(2,1)S(1)}, bf16[4096,1024]{1,0:T(8,128)(2,1)S(1)}, bf16[1024,4096]{1,0:T(8,128)(2,1)S(1)}) custom-call(bf16[4096,1024]{1,0:T(8,128)(2,1)} %refs_0_.6, bf16[4096,1024]{1,0:T(8,128)(2,1)} %refs_1_, bf16[1024,4096]{1,0:T(8,128)(2,1)} %refs_2_), custom_call_target="tpu_custom_call" | custom-call | flops 3221225472 | bytes 25165824 | tf_op jit(solution)/shard_map/pallas_call | solution.py:282
  14.2 1.6 collective-permute-done.1.refs_2_
  16.0 2.3 %shard_map.97 = bf16[8,1,1,128,128]{4,3,2,1,0:T(8,128)(2,1)S(1)} custom-call(bf16[32,4096]{1,0:T(8,128)(2,1)S(1)} %copy-done.2, bf16[32,4096]{1,0:T(8,128)(2,1)S(1)} %collective-permute-done.3.refs_1_, bf16[32,4096]{1,0:T(8,128)(2,1)S(1)} %collective-permute-done.4.refs_2_, bf16[32,4096]{1,0:T(8,128)(2,1)S(1)} %collective-permute-done.5.refs_3_, ...), custom_call_target="tpu_custom_call" | custom-call | flops 1073741824 | bytes 8388608 | tf_op jit(solution)/shard_map/pallas_call | solution.py:308
  18.4 5.0 %shard_map.96 = (bf16[8,3,1,128,128]{4,3,2,1,0:T(8,128)(2,1)S(1)}, f32[128,128]{1,0:T(8,128)S(1)}, bf16[4096,1024]{1,0:T(8,128)(2,1)S(1)}) custom-call(bf16[32,4096]{1,0:T(8,128)(2,1)S(1)} %copy-done.1, bf16[32,4096]{1,0:T(8,128)(2,1)S(1)} %collective-permute-done.refs_1_, bf16[32,4096]{1,0:T(8,128)(2,1)S(1)} %collective-permute-done.1.refs_2_, ...), custom_call_target="tpu_custom_call" | custom-call | flops 3221225472 | bytes 25165824 | tf_op jit(solution)/shard_map/pallas_call | solution.py:360
  23.5 32.3 %all_to_all.20.qkv_ref.g_ref = bf16[8,4,1,128,128]{4,3,2,1,0:T(8,128)(2,1)S(1)} all-to-all(bf16[8,4,1,128,128]{4,3,2,1,0:T(8,128)(2,1)S(1)} %pad_maximum_fusion), channel_id=1, replica_groups=mesh['seq'=8,'tensor'=4] {'seq'}, dimensions={0} | all-to-all | bytes 2097152 | tf_op jit(solution)/shard_map/all_to_all | solution.py:230
  55.8 5.4 %shard_map.98 = (bf16[8,3,1,128,128]{4,3,2,1,0:T(8,128)(2,1)S(1)}, f32[1,1024,1024]{2,1,0:T(8,128)S(1)}, bf16[1,128,1024]{2,1,0:T(8,128)(2,1)S(1)}) custom-call(s32[1]{0:T(128)} %bitcast.1.flip_ref, s32[16,16]{1,0:T(8,128)S(1)} %copy-done.4, bf16[8,4,1,128,128]{4,3,2,1,0:T(8,128)(2,1)S(1)} %all_to_all.20.qkv_ref.g_ref, ...), custom_call_target="tpu_custom_call" | custom-call | flops 1610612736 | bytes 2097152 | tf_op jit(solution)/shard_map/pallas_call | solution.py:569
  61.2 23.7 %all_to_all.21.refs_5_ = bf16[8,3,1,128,128]{4,3,2,1,0:T(8,128)(2,1)S(1)} all-to-all(bf16[8,3,1,128,128]{4,3,2,1,0:T(8,128)(2,1)S(1)} %get-tuple-element.55), channel_id=1, replica_groups=mesh['seq'=8,'tensor'=4] {'seq'}, dimensions={0} | all-to-all | bytes 1572864 | tf_op jit(solution)/shard_map/all_to_all | solution.py:230
  84.9 3.6 %shard_map.100 = (bf16[32,2048]{1,0:T(8,128)(2,1)S(1)}, bf16[32,2048]{1,0:T(8,128)(2,1)S(1)}, bf16[32,2048]{1,0:T(8,128)(2,1)S(1)}, bf16[32,2048]{1,0:T(8,128)(2,1)S(1)}, f32[1,2048]{1,0:T(1,128)S(1)}) custom-call(bf16[32,4096]{1,0:T(8,128)(2,1)S(1)} %copy-done.1, bf16[32,4096]{1,0:T(8,128)(2,1)S(1)} %collective-permute-done.refs_1_, ...), custom_call_target="tpu_custom_call" | custom-call | flops 1610612736 | bytes 12582912 | tf_op jit(solution)/shard_map/pallas_call | solution.py:418
  89.1 3.6 %shard_map.99 = (bf16[32,2048]{1,0:T(8,128)(2,1)S(1)}, bf16[32,2048]{1,0:T(8,128)(2,1)S(1)}, bf16[32,2048]{1,0:T(8,128)(2,1)S(1)}, bf16[32,2048]{1,0:T(8,128)(2,1)S(1)}, f32[1,2048]{1,0:T(1,128)S(1)}) custom-call(bf16[32,4096]{1,0:T(8,128)(2,1)S(1)} %copy-done.1, bf16[32,4096]{1,0:T(8,128)(2,1)S(1)} %collective-permute-done.refs_1_, ...), custom_call_target="tpu_custom_call" | custom-call | flops 1610612736 | bytes 12582912 | tf_op jit(solution)/shard_map/pallas_call | solution.py:418
  93.2 1.6 collective-permute-start.11
  95.8 3.8 %collective-permute-done.11.refs_5_ = bf16[32,2048]{1,0:T(8,128)(2,1)S(1)} collective-permute-done((bf16[32,2048]{1,0:T(8,128)(2,1)S(1)}, bf16[32,2048]{1,0:T(8,128)(2,1)S(1)}, u32[]{:S(2)}, u32[]{:S(2)}) %collective-permute-start.11) | collective-permute-done | bytes 131104 | tf_op jit(solution)/shard_map/ppermute | solution.py:208
  99.7 1.9 %collective-permute-done.8.refs_2_ = bf16[32,2048]{1,0:T(8,128)(2,1)S(1)} collective-permute-done((bf16[32,2048]{1,0:T(8,128)(2,1)S(1)}, bf16[32,2048]{1,0:T(8,128)(2,1)S(1)}, u32[]{:S(2)}, u32[]{:S(2)}) %collective-permute-start.8) | collective-permute-done | bytes 131104 | tf_op jit(solution)/shard_map/ppermute | solution.py:208
  101.9 1.6 collective-permute-start.13
  103.5 5.9 %collective-permute-done.13.refs_2_ = bf16[32,4096]{1,0:T(8,128)(2,1)S(1)} collective-permute-done((bf16[32,4096]{1,0:T(8,128)(2,1)S(1)}, bf16[32,4096]{1,0:T(8,128)(2,1)S(1)}, u32[]{:S(2)}, u32[]{:S(2)}) %collective-permute-start.13) | collective-permute-done | bytes 262176 | tf_op jit(solution)/shard_map/ppermute | solution.py:192
  109.5 1.5 collective-permute-done.14.refs_3_
  111.0 2.3 %shard_map.102 = bf16[8,1,1,128,128]{4,3,2,1,0:T(8,128)(2,1)S(1)} custom-call(bf16[32,4096]{1,0:T(8,128)(2,1)S(1)} %get-tuple-element.65.refs_0_, bf16[32,4096]{1,0:T(8,128)(2,1)S(1)} %collective-permute-done.12.refs_1_, bf16[32,4096]{1,0:T(8,128)(2,1)S(1)} %collective-permute-done.13.refs_2_, bf16[32,4096]{1,0:T(8,128)(2,1)S(1)} %collective-permute-done.14.refs_3_, ...), custom_call_target="tpu_custom_call" | custom-call | flops 1073741824 | bytes 8388608 | tf_op jit(solution)/shard_map/pallas_call | solution.py:308
  113.3 12.7 %all_to_all.22.g_ref = bf16[8,1,1,128,128]{4,3,2,1,0:T(8,128)(2,1)S(1)} all-to-all(bf16[8,1,1,128,128]{4,3,2,1,0:T(8,128)(2,1)S(1)} %shard_map.102), channel_id=1, replica_groups=mesh['seq'=8,'tensor'=4] {'seq'}, dimensions={0} | all-to-all | bytes 524288 | tf_op jit(solution)/shard_map/all_to_all | solution.py:230
  126.0 1.8 shard_map.103
  127.7 23.2 %all_to_all.23.refs_5_ = bf16[8,3,1,128,128]{4,3,2,1,0:T(8,128)(2,1)S(1)} all-to-all(bf16[8,3,1,128,128]{4,3,2,1,0:T(8,128)(2,1)S(1)} %shard_map.103), channel_id=1, replica_groups=mesh['seq'=8,'tensor'=4] {'seq'}, dimensions={0} | all-to-all | bytes 1572864 | tf_op jit(solution)/shard_map/all_to_all | solution.py:230
  150.9 3.6 %shard_map.105 = (bf16[32,2048]{1,0:T(8,128)(2,1)S(1)}, bf16[32,2048]{1,0:T(8,128)(2,1)S(1)}, bf16[32,2048]{1,0:T(8,128)(2,1)S(1)}, bf16[32,2048]{1,0:T(8,128)(2,1)S(1)}, f32[1,2048]{1,0:T(1,128)S(1)}) custom-call(bf16[32,4096]{1,0:T(8,128)(2,1)S(1)} %copy-done.1, bf16[32,4096]{1,0:T(8,128)(2,1)S(1)} %collective-permute-done.refs_1_, ...), custom_call_target="tpu_custom_call" | custom-call | flops 1610612736 | bytes 12582912 | tf_op jit(solution)/shard_map/pallas_call | solution.py:418
  154.5 3.6 %shard_map.104 = (bf16[32,2048]{1,0:T(8,128)(2,1)S(1)}, bf16[32,2048]{1,0:T(8,128)(2,1)S(1)}, bf16[32,2048]{1,0:T(8,128)(2,1)S(1)}, bf16[32,2048]{1,0:T(8,128)(2,1)S(1)}, f32[1,2048]{1,0:T(1,128)S(1)}) custom-call(bf16[32,4096]{1,0:T(8,128)(2,1)S(1)} %copy-done.1, bf16[32,4096]{1,0:T(8,128)(2,1)S(1)} %collective-permute-done.refs_1_, ...), custom_call_target="tpu_custom_call" | custom-call | flops 1610612736 | bytes 12582912 | tf_op jit(solution)/shard_map/pallas_call | solution.py:418
  158.2 1.2 collective-permute-done.21
  159.3 1.1 collective-permute-start.24
  160.5 1.4 collective-permute-start.23
  161.9 1.8 %collective-permute-start.22 = (f32[4096]{0:T(1024)S(1)}, f32[4096]{0:T(1024)S(1)}, u32[]{:S(2)}, u32[]{:S(2)}) collective-permute-start(f32[4096]{0:T(1024)S(1)} %add.49), channel_id=1, source_target_pairs={{0,8},{1,9},{2,10},{3,11},{4,12},{5,13},{6,14},{7,15},{8,0},{9,1},... | collective-permute-start | bytes 49160 | tf_op jit(solution)/shard_map/ppermute | solution.py:222
  165.7 2.4 %collective-permute-start.27 = (f32[4096]{0:T(1024)S(1)}, f32[4096]{0:T(1024)S(1)}, u32[]{:S(2)}, u32[]{:S(2)}) collective-permute-start(f32[4096]{0:T(1024)S(1)} %add_add_fusion), channel_id=1, source_target_pairs={{0,6},{1,7},{2,4},{3,5},{4,2},{5,3},{6,0},{7,1},{8,14},{9,15},{10,... | collective-permute-start | bytes 49160 | tf_op jit(solution)/shard_map/ppermute | solution.py:222
  169.4 1.0 collective-permute-done.27
  170.4 1.5 collective-permute-start.20
  173.3 3.0 %collective-permute-done.20.refs_5_ = bf16[32,2048]{1,0:T(8,128)(2,1)S(1)} collective-permute-done((bf16[32,2048]{1,0:T(8,128)(2,1)S(1)}, bf16[32,2048]{1,0:T(8,128)(2,1)S(1)}, u32[]{:S(2)}, u32[]{:S(2)}) %collective-permute-start.20) | collective-permute-done | bytes 131104 | tf_op jit(solution)/shard_map/ppermute | solution.py:208
  176.3 1.4 collective-permute-done.17.refs_2_
  177.7 1.2 shard_map.106
  (71 shorter events, 9.6 us)
Async XLA Ops:
  0.6 13.0 %collective-permute-start.4 = (bf16[32,4096]{1,0:T(8,128)(2,1)}, bf16[32,4096]{1,0:T(8,128)(2,1)S(1)}, u32[]{:S(2)}, u32[]{:S(2)}) collective-permute-start(bf16[32,4096]{1,0:T(8,128)(2,1)} %refs_9_.3), channel_id=1, source_target_pairs={{0,2},{1,3},{2,0},{3,1},{4,6},{5,7},{6,4},{7,5},{8,10},{9,11},{10,... | collective-permute-start | bytes 786440 | tf_op jit(solution)/shard_map/ppermute | solution.py:192
  3.7 12.3 %collective-permute-start.3 = (bf16[32,4096]{1,0:T(8,128)(2,1)}, bf16[32,4096]{1,0:T(8,128)(2,1)S(1)}, u32[]{:S(2)}, u32[]{:S(2)}) collective-permute-start(bf16[32,4096]{1,0:T(8,128)(2,1)} %refs_9_.3), channel_id=1, source_target_pairs={{0,1},{1,0},{2,3},{3,2},{4,5},{5,4},{6,7},{7,6},{8,9},{9,8},{10,11... | collective-permute-start | bytes 786440 | tf_op jit(solution)/shard_map/ppermute | solution.py:192
  3.7 12.1 %collective-permute-start.1 = (bf16[32,4096]{1,0:T(8,128)(2,1)}, bf16[32,4096]{1,0:T(8,128)(2,1)S(1)}, u32[]{:S(2)}, u32[]{:S(2)}) collective-permute-start(bf16[32,4096]{1,0:T(8,128)(2,1)} %refs_6_.3), channel_id=1, source_target_pairs={{0,2},{1,3},{2,0},{3,1},{4,6},{5,7},{6,4},{7,5},{8,10},{9,11},{10,... | collective-permute-start | bytes 786440 | tf_op jit(solution)/shard_map/ppermute | solution.py:192
  3.8 14.5 %collective-permute-start = (bf16[32,4096]{1,0:T(8,128)(2,1)}, bf16[32,4096]{1,0:T(8,128)(2,1)S(1)}, u32[]{:S(2)}, u32[]{:S(2)}) collective-permute-start(bf16[32,4096]{1,0:T(8,128)(2,1)} %refs_6_.3), channel_id=1, source_target_pairs={{0,1},{1,0},{2,3},{3,2},{4,5},{5,4},{6,7},{7,6},{8,9},{9,8},{10,11... | collective-permute-start | bytes 786440 | tf_op jit(solution)/shard_map/ppermute | solution.py:192
  4.2 11.8 %copy-start.2 = (bf16[32,4096]{1,0:T(8,128)(2,1)S(1)}, bf16[32,4096]{1,0:T(8,128)(2,1)}, u32[]{:S(2)}) copy-start(bf16[32,4096]{1,0:T(8,128)(2,1)} %refs_9_.3) | copy-start | bytes 786436
  13.6 2.4 %collective-permute-start.5 = (bf16[32,4096]{1,0:T(8,128)(2,1)S(1)}, bf16[32,4096]{1,0:T(8,128)(2,1)S(1)}, u32[]{:S(2)}, u32[]{:S(2)}) collective-permute-start(bf16[32,4096]{1,0:T(8,128)(2,1)S(1)} %collective-permute-done.4.refs_2_), channel_id=1, source_target_pairs={{0,1},{1,0},{2,3},{3,2},{4,5},{5,4},{6,7},{7,6},{8,9},{9,8},{10,11... | collective-permute-start | bytes 786440 | tf_op jit(solution)/shard_map/ppermute | solution.py:192
  15.8 2.6 %collective-permute-start.2 = (bf16[32,4096]{1,0:T(8,128)(2,1)S(1)}, bf16[32,4096]{1,0:T(8,128)(2,1)S(1)}, u32[]{:S(2)}, u32[]{:S(2)}) collective-permute-start(bf16[32,4096]{1,0:T(8,128)(2,1)S(1)} %collective-permute-done.1.refs_2_), channel_id=1, source_target_pairs={{0,1},{1,0},{2,3},{3,2},{4,5},{5,4},{6,7},{7,6},{8,9},{9,8},{10,11... | collective-permute-start | bytes 786440 | tf_op jit(solution)/shard_map/ppermute | solution.py:192
  18.4 37.4 %copy-start.4 = (s32[16,16]{1,0:T(8,128)S(1)}, s32[16,16]{1,0:T(8,128)}, u32[]{:S(2)}) copy-start(s32[16,16]{1,0:T(8,128)} %layout_ref.3) | copy-start | bytes 3076
  88.5 7.3 %collective-permute-start.9 = (bf16[32,2048]{1,0:T(8,128)(2,1)S(1)}, bf16[32,2048]{1,0:T(8,128)(2,1)S(1)}, u32[]{:S(2)}, u32[]{:S(2)}) collective-permute-start(bf16[32,2048]{1,0:T(8,128)(2,1)S(1)} %get-tuple-element.62), channel_id=1, source_target_pairs={{0,1},{1,0},{2,3},{3,2},{4,5},{5,4},{6,7},{7,6},{8,9},{9,8},{10,11... | collective-permute-start | bytes 393224 | tf_op jit(solution)/shard_map/ppermute | solution.py:208
  88.6 22.4 %slice-start = ((s8[8388608]{0:T(1024)(128)(4,1)}), s8[4194304]{0:T(1024)(128)(4,1)S(1)}, s32[]{:S(2)}) async-start(s8[8388608]{0:T(1024)(128)(4,1)} %bitcast.6), calls=%async_computation.4 | async-start | bytes 8388608
  88.6 22.4 %slice-start.1 = ((s8[8388608]{0:T(1024)(128)(4,1)}), s8[4194304]{0:T(1024)(128)(4,1)S(1)}, s32[]{:S(2)}) async-start(s8[8388608]{0:T(1024)(128)(4,1)} %bitcast.6), calls=%async_computation.5 | async-start | bytes 8388608
  88.6 4.6 %collective-permute-start.10 = (bf16[32,2048]{1,0:T(8,128)(2,1)S(1)}, bf16[32,2048]{1,0:T(8,128)(2,1)S(1)}, u32[]{:S(2)}, u32[]{:S(2)}) collective-permute-start(bf16[32,2048]{1,0:T(8,128)(2,1)S(1)} %get-tuple-element.64), channel_id=1, source_target_pairs={{0,1},{1,0},{2,3},{3,2},{4,5},{5,4},{6,7},{7,6},{8,9},{9,8},{10,11... | collective-permute-start | bytes 393224 | tf_op jit(solution)/shard_map/ppermute | solution.py:208
  92.6 3.2 %collective-permute-start.6 = (bf16[32,2048]{1,0:T(8,128)(2,1)S(1)}, bf16[32,2048]{1,0:T(8,128)(2,1)S(1)}, u32[]{:S(2)}, u32[]{:S(2)}) collective-permute-start(bf16[32,2048]{1,0:T(8,128)(2,1)S(1)} %get-tuple-element.58), channel_id=1, source_target_pairs={{0,1},{1,0},{2,3},{3,2},{4,5},{5,4},{6,7},{7,6},{8,9},{9,8},{10,11... | collective-permute-start | bytes 393224 | tf_op jit(solution)/shard_map/ppermute | solution.py:208
  92.8 2.0 %collective-permute-start.7 = (bf16[32,2048]{1,0:T(8,128)(2,1)S(1)}, bf16[32,2048]{1,0:T(8,128)(2,1)S(1)}, u32[]{:S(2)}, u32[]{:S(2)}) collective-permute-start(bf16[32,2048]{1,0:T(8,128)(2,1)S(1)} %get-tuple-element.60), channel_id=1, source_target_pairs={{0,1},{1,0},{2,3},{3,2},{4,5},{5,4},{6,7},{7,6},{8,9},{9,8},{10,11... | collective-permute-start | bytes 393224 | tf_op jit(solution)/shard_map/ppermute | solution.py:208
  93.2 6.4 %collective-permute-start.11 = (bf16[32,2048]{1,0:T(8,128)(2,1)S(1)}, bf16[32,2048]{1,0:T(8,128)(2,1)S(1)}, u32[]{:S(2)}, u32[]{:S(2)}) collective-permute-start(bf16[32,2048]{1,0:T(8,128)(2,1)S(1)} %add_convert_fusion.2), channel_id=1, source_target_pairs={{0,2},{1,3},{2,0},{3,1},{4,6},{5,7},{6,4},{7,5},{8,10},{9,11},{10,... | collective-permute-start | bytes 393224 | tf_op jit(solution)/shard_map/ppermute | solution.py:208
  94.8 6.8 %collective-permute-start.8 = (bf16[32,2048]{1,0:T(8,128)(2,1)S(1)}, bf16[32,2048]{1,0:T(8,128)(2,1)S(1)}, u32[]{:S(2)}, u32[]{:S(2)}) collective-permute-start(bf16[32,2048]{1,0:T(8,128)(2,1)S(1)} %add_convert_fusion.3), channel_id=1, source_target_pairs={{0,2},{1,3},{2,0},{3,1},{4,6},{5,7},{6,4},{7,5},{8,10},{9,11},{10,... | collective-permute-start | bytes 393224 | tf_op jit(solution)/shard_map/ppermute | solution.py:208
  101.9 7.5 %collective-permute-start.13 = (bf16[32,4096]{1,0:T(8,128)(2,1)S(1)}, bf16[32,4096]{1,0:T(8,128)(2,1)S(1)}, u32[]{:S(2)}, u32[]{:S(2)}) collective-permute-start(bf16[32,4096]{1,0:T(8,128)(2,1)S(1)} %get-tuple-element.65.refs_0_), channel_id=1, source_target_pairs={{0,2},{1,3},{2,0},{3,1},{4,6},{5,7},{6,4},{7,5},{8,10},{9,11},{10,... | collective-permute-start | bytes 786440 | tf_op jit(solution)/shard_map/ppermute | solution.py:192
  103.5 6.0 %collective-permute-start.12 = (bf16[32,4096]{1,0:T(8,128)(2,1)S(1)}, bf16[32,4096]{1,0:T(8,128)(2,1)S(1)}, u32[]{:S(2)}, u32[]{:S(2)}) collective-permute-start(bf16[32,4096]{1,0:T(8,128)(2,1)S(1)} %get-tuple-element.65.refs_0_), channel_id=1, source_target_pairs={{0,1},{1,0},{2,3},{3,2},{4,5},{5,4},{6,7},{7,6},{8,9},{9,8},{10,11... | collective-permute-start | bytes 786440 | tf_op jit(solution)/shard_map/ppermute | solution.py:192
  109.4 1.5 collective-permute-start.14
  158.1 1.2 collective-permute-start.21
  159.3 5.5 %collective-permute-start.24 = (f32[4096]{0:T(1024)S(1)}, f32[4096]{0:T(1024)S(1)}, u32[]{:S(2)}, u32[]{:S(2)}) collective-permute-start(f32[4096]{0:T(1024)S(1)} %add.49), channel_id=1, source_target_pairs={{0,24},{1,25},{2,26},{3,27},{4,28},{5,29},{6,30},{7,31},{8,16},{9,... | collective-permute-start | bytes 49160 | tf_op jit(solution)/shard_map/ppermute | solution.py:222
  160.5 4.8 %collective-permute-start.23 = (f32[4096]{0:T(1024)S(1)}, f32[4096]{0:T(1024)S(1)}, u32[]{:S(2)}, u32[]{:S(2)}) collective-permute-start(f32[4096]{0:T(1024)S(1)} %add.49), channel_id=1, source_target_pairs={{0,16},{1,17},{2,18},{3,19},{4,20},{5,21},{6,22},{7,23},{8,24},{9,... | collective-permute-start | bytes 49160 | tf_op jit(solution)/shard_map/ppermute | solution.py:222
  161.9 3.7 %collective-permute-start.22 = (f32[4096]{0:T(1024)S(1)}, f32[4096]{0:T(1024)S(1)}, u32[]{:S(2)}, u32[]{:S(2)}) collective-permute-start(f32[4096]{0:T(1024)S(1)} %add.49), channel_id=1, source_target_pairs={{0,8},{1,9},{2,10},{3,11},{4,12},{5,13},{6,14},{7,15},{8,0},{9,1},... | collective-permute-start | bytes 49160 | tf_op jit(solution)/shard_map/ppermute | solution.py:222
  163.7 9.6 %collective-permute-start.18 = (bf16[32,2048]{1,0:T(8,128)(2,1)S(1)}, bf16[32,2048]{1,0:T(8,128)(2,1)S(1)}, u32[]{:S(2)}, u32[]{:S(2)}) collective-permute-start(bf16[32,2048]{1,0:T(8,128)(2,1)S(1)} %get-tuple-element.73), channel_id=1, source_target_pairs={{0,1},{1,0},{2,3},{3,2},{4,5},{5,4},{6,7},{7,6},{8,9},{9,8},{10,11... | collective-permute-start | bytes 393224 | tf_op jit(solution)/shard_map/ppermute | solution.py:208
  163.7 4.3 %collective-permute-start.19 = (bf16[32,2048]{1,0:T(8,128)(2,1)S(1)}, bf16[32,2048]{1,0:T(8,128)(2,1)S(1)}, u32[]{:S(2)}, u32[]{:S(2)}) collective-permute-start(bf16[32,2048]{1,0:T(8,128)(2,1)S(1)} %get-tuple-element.75), channel_id=1, source_target_pairs={{0,1},{1,0},{2,3},{3,2},{4,5},{5,4},{6,7},{7,6},{8,9},{9,8},{10,11... | collective-permute-start | bytes 393224 | tf_op jit(solution)/shard_map/ppermute | solution.py:208
  164.9 8.5 %collective-permute-start.15 = (bf16[32,2048]{1,0:T(8,128)(2,1)S(1)}, bf16[32,2048]{1,0:T(8,128)(2,1)S(1)}, u32[]{:S(2)}, u32[]{:S(2)}) collective-permute-start(bf16[32,2048]{1,0:T(8,128)(2,1)S(1)} %get-tuple-element.69), channel_id=1, source_target_pairs={{0,1},{1,0},{2,3},{3,2},{4,5},{5,4},{6,7},{7,6},{8,9},{9,8},{10,11... | collective-permute-start | bytes 393224 | tf_op jit(solution)/shard_map/ppermute | solution.py:208
  165.2 3.5 %collective-permute-start.16 = (bf16[32,2048]{1,0:T(8,128)(2,1)S(1)}, bf16[32,2048]{1,0:T(8,128)(2,1)S(1)}, u32[]{:S(2)}, u32[]{:S(2)}) collective-permute-start(bf16[32,2048]{1,0:T(8,128)(2,1)S(1)} %get-tuple-element.71), channel_id=1, source_target_pairs={{0,1},{1,0},{2,3},{3,2},{4,5},{5,4},{6,7},{7,6},{8,9},{9,8},{10,11... | collective-permute-start | bytes 393224 | tf_op jit(solution)/shard_map/ppermute | solution.py:208
  165.7 4.7 %collective-permute-start.27 = (f32[4096]{0:T(1024)S(1)}, f32[4096]{0:T(1024)S(1)}, u32[]{:S(2)}, u32[]{:S(2)}) collective-permute-start(f32[4096]{0:T(1024)S(1)} %add_add_fusion), channel_id=1, source_target_pairs={{0,6},{1,7},{2,4},{3,5},{4,2},{5,3},{6,0},{7,1},{8,14},{9,15},{10,... | collective-permute-start | bytes 49160 | tf_op jit(solution)/shard_map/ppermute | solution.py:222
  168.0 3.8 %collective-permute-start.26 = (f32[4096]{0:T(1024)S(1)}, f32[4096]{0:T(1024)S(1)}, u32[]{:S(2)}, u32[]{:S(2)}) collective-permute-start(f32[4096]{0:T(1024)S(1)} %add_add_fusion), channel_id=1, source_target_pairs={{0,4},{1,5},{2,6},{3,7},{4,0},{5,1},{6,2},{7,3},{8,12},{9,13},{10,... | collective-permute-start | bytes 49160 | tf_op jit(solution)/shard_map/ppermute | solution.py:222
  168.7 4.0 %collective-permute-start.25 = (f32[4096]{0:T(1024)S(1)}, f32[4096]{0:T(1024)S(1)}, u32[]{:S(2)}, u32[]{:S(2)}) collective-permute-start(f32[4096]{0:T(1024)S(1)} %add_add_fusion), channel_id=1, source_target_pairs={{0,2},{1,3},{2,0},{3,1},{4,6},{5,7},{6,4},{7,5},{8,10},{9,11},{10,... | collective-permute-start | bytes 49160 | tf_op jit(solution)/shard_map/ppermute | solution.py:222
  170.4 5.9 %collective-permute-start.20 = (bf16[32,2048]{1,0:T(8,128)(2,1)S(1)}, bf16[32,2048]{1,0:T(8,128)(2,1)S(1)}, u32[]{:S(2)}, u32[]{:S(2)}) collective-permute-start(bf16[32,2048]{1,0:T(8,128)(2,1)S(1)} %add_convert_fusion), channel_id=1, source_target_pairs={{0,2},{1,3},{2,0},{3,1},{4,6},{5,7},{6,4},{7,5},{8,10},{9,11},{10,... | collective-permute-start | bytes 393224 | tf_op jit(solution)/shard_map/ppermute | solution.py:208
  171.9 5.8 %collective-permute-start.17 = (bf16[32,2048]{1,0:T(8,128)(2,1)S(1)}, bf16[32,2048]{1,0:T(8,128)(2,1)S(1)}, u32[]{:S(2)}, u32[]{:S(2)}) collective-permute-start(bf16[32,2048]{1,0:T(8,128)(2,1)S(1)} %add_convert_fusion.1), channel_id=1, source_target_pairs={{0,2},{1,3},{2,0},{3,1},{4,6},{5,7},{6,4},{7,5},{8,10},{9,11},{10,... | collective-permute-start | bytes 393224 | tf_op jit(solution)/shard_map/ppermute | solution.py:208
  (3 other events, 22.3 us)

commit v3 on v2

--- a/solution.py
+++ b/solution.py
@@ -187,12 +187,10 @@
     blocks = {0: block}
     distance = lax.axis_size("tensor") // 2
     while distance:
-        blocks.update(
-            {
-                j ^ distance: lax.ppermute(b, "tensor", xor_pairs("tensor", distance))
-                for j, b in list(blocks.items())
-            }
-        )
+        for j, held in list(blocks.items()):
+            blocks[j ^ distance] = lax.ppermute(
+                held, "tensor", xor_pairs("tensor", distance)
+            )
         distance //= 2
     return [blocks[j] for j in range(len(blocks))]
 
@@ -510,12 +508,17 @@
         chosen = contract(
             key_rows, query_hot.astype(jnp.float32).astype(jnp.bfloat16), 1, 0
         )
+        key_pos, query_pos = key_pos[start:], query_pos[start:]
         key_block, query_block = key_pos // BLK, query_pos // BLK
-        allowed = ((key_block < query_block) & (chosen > 0.5)) | (
+        near = ((key_block < query_block) & (chosen[start:] > 0.5)) | (
             (key_block == query_block) & (key_pos <= query_pos)
         )
         scores = contract(keys[:seen], query, 1, 1) * scale
-        scores = jnp.where(allowed, scores, MASKED)
+        square = jnp.where(near, scores[start:], MASKED)
+        if start:
+            earlier = jnp.where(chosen[:start] > 0.5, scores[:start], MASKED)
+            square = jnp.concatenate([earlier, square], axis=0)
+        scores = square
         probs = jnp.exp(scores - jnp.max(scores, axis=0, keepdims=True))
         return probs * (1.0 / jnp.sum(probs, axis=0, keepdims=True))
 
@@ -610,7 +613,8 @@
     half = HEAD_DIM // 2
     own_sine = jnp.concatenate([own_sine[:, :half], -own_sine[:, half:]], axis=1)
 
-    points, grad_pieces = xor_gather(fixed_point), xor_gather(incoming)
+    points = xor_gather(fixed_point)
+    grad_pieces = xor_gather(incoming)
     sent, inverse, value_weight = project(
         points, norm_gain, own_cosine, own_sine, (*weights, value_weight), seq
     )

time: 179 us -> 179 us (level)
  no operation moved by 1% of the time
where the time goes in v3:
time: 179 us
  blocking collectives  91.9 us (51%)
  Pallas kernels  40.8 us (23%)
  waiting for transfers between devices  23 us (13%)
  starting transfers between devices  19.8 us (11%)
  other arithmetic  2.34 us (1%)
    all_to_all x4, blocking collectives, swap(): lax.all_to_all(values, 'seq', split_axis=0, concat_axis=0, tiled=True)  91.9 us
    pallas_call x4, Pallas kernels, combine(): pl.pallas_call(functools.partial(combine_kernel, pieces=len(points), colu...  14.3 us
    ppermute x12, waiting for transfers between devices, xor_reduce_scatter(): lax.ppermute(parts[0], 'tensor', xor_pairs('tensor', distance))  10.2 us
    ppermute x9, waiting for transfers between devices, xor_gather(): lax.ppermute(held, 'tensor', xor_pairs('tensor', distance))  9.11 us
    pallas_call x1, Pallas kernels, load(): pl.pallas_call(functools.partial(load_kernel, count=len(weights)), out_sh...  8.38 us
    ppermute x7, starting transfers between devices, all_sum(): lax.ppermute(values, axes, [(i, i ^ distance) for i in range(size)])  8.07 us
    pallas_call x2, Pallas kernels, attention_grads(): pl.pallas_call(functools.partial(attention_kernel, step=min(max(256, rows...  7.01 us
    ppermute x12, starting transfers between devices, xor_reduce_scatter(): lax.ppermute(parts[0], 'tensor', xor_pairs('tensor', distance))  6.34 us
  transfers between devices with their start and end apart: 28, of which 13 were waited for; matrix products, arithmetic and copies ran while one was open for 1% of the time, Pallas kernels for 8%

profile of v3, /device:TPU:0, one launch (start us, length us, event | category | flops | bytes accessed | tf_op | source)
XLA Modules:
  0.0 178.7 jit_solution(10961276070278689386)
XLA Ops:
  0.6 3.0 %collective-permute-start.4 = (bf16[32,4096]{1,0:T(8,128)(2,1)}, bf16[32,4096]{1,0:T(8,128)(2,1)S(1)}, u32[]{:S(2)}, u32[]{:S(2)}) collective-permute-start(bf16[32,4096]{1,0:T(8,128)(2,1)} %refs_9_.3), channel_id=1, source_target_pairs={{0,2},{1,3},{2,0},{3,1},{4,6},{5,7},{6,4},{7,5},{8,10},{9,11},{10,... | collective-permute-start | bytes 786440 | tf_op jit(solution)/shard_map/ppermute | solution.py:191
  4.2 8.4 %shard_map.95 = (bf16[4096,1024]{1,0:T(8,128)(2,1)S(1)}, bf16[4096,1024]{1,0:T(8,128)(2,1)S(1)}, bf16[1024,4096]{1,0:T(8,128)(2,1)S(1)}) custom-call(bf16[4096,1024]{1,0:T(8,128)(2,1)} %refs_0_.6, bf16[4096,1024]{1,0:T(8,128)(2,1)} %refs_1_, bf16[1024,4096]{1,0:T(8,128)(2,1)} %refs_2_), custom_call_target="tpu_custom_call" | custom-call | flops 3221225472 | bytes 25165824 | tf_op jit(solution)/shard_map/pallas_call | solution.py:280
  14.2 1.6 collective-permute-done.1.refs_2_
  16.0 2.3 %shard_map.97 = bf16[8,1,1,128,128]{4,3,2,1,0:T(8,128)(2,1)S(1)} custom-call(bf16[32,4096]{1,0:T(8,128)(2,1)S(1)} %copy-done.2, bf16[32,4096]{1,0:T(8,128)(2,1)S(1)} %collective-permute-done.3.refs_1_, bf16[32,4096]{1,0:T(8,128)(2,1)S(1)} %collective-permute-done.4.refs_2_, bf16[32,4096]{1,0:T(8,128)(2,1)S(1)} %collective-permute-done.5.refs_3_, ...), custom_call_target="tpu_custom_call" | custom-call | flops 1073741824 | bytes 8388608 | tf_op jit(solution)/shard_map/pallas_call | solution.py:306
  18.4 5.0 %shard_map.96 = (bf16[8,3,1,128,128]{4,3,2,1,0:T(8,128)(2,1)S(1)}, f32[128,128]{1,0:T(8,128)S(1)}, bf16[4096,1024]{1,0:T(8,128)(2,1)S(1)}) custom-call(bf16[32,4096]{1,0:T(8,128)(2,1)S(1)} %copy-done.1, bf16[32,4096]{1,0:T(8,128)(2,1)S(1)} %collective-permute-done.refs_1_, bf16[32,4096]{1,0:T(8,128)(2,1)S(1)} %collective-permute-done.1.refs_2_, ...), custom_call_target="tpu_custom_call" | custom-call | flops 3221225472 | bytes 25165824 | tf_op jit(solution)/shard_map/pallas_call | solution.py:358
  23.5 32.3 %all_to_all.20.qkv_ref.g_ref = bf16[8,4,1,128,128]{4,3,2,1,0:T(8,128)(2,1)S(1)} all-to-all(bf16[8,4,1,128,128]{4,3,2,1,0:T(8,128)(2,1)S(1)} %pad_maximum_fusion), channel_id=1, replica_groups=mesh['seq'=8,'tensor'=4] {'seq'}, dimensions={0} | all-to-all | bytes 2097152 | tf_op jit(solution)/shard_map/all_to_all | solution.py:228
  55.8 5.2 %shard_map.98 = (bf16[8,3,1,128,128]{4,3,2,1,0:T(8,128)(2,1)S(1)}, f32[1,1024,1024]{2,1,0:T(8,128)S(1)}, bf16[1,128,1024]{2,1,0:T(8,128)(2,1)S(1)}) custom-call(s32[1]{0:T(128)} %bitcast.1.flip_ref, s32[16,16]{1,0:T(8,128)S(1)} %copy-done.4, bf16[8,4,1,128,128]{4,3,2,1,0:T(8,128)(2,1)S(1)} %all_to_all.20.qkv_ref.g_ref, ...), custom_call_target="tpu_custom_call" | custom-call | flops 1610612736 | bytes 2097152 | tf_op jit(solution)/shard_map/pallas_call | solution.py:572
  61.0 23.7 %all_to_all.21.refs_5_ = bf16[8,3,1,128,128]{4,3,2,1,0:T(8,128)(2,1)S(1)} all-to-all(bf16[8,3,1,128,128]{4,3,2,1,0:T(8,128)(2,1)S(1)} %get-tuple-element.55), channel_id=1, replica_groups=mesh['seq'=8,'tensor'=4] {'seq'}, dimensions={0} | all-to-all | bytes 1572864 | tf_op jit(solution)/shard_map/all_to_all | solution.py:228
  84.7 3.6 %shard_map.100 = (bf16[32,2048]{1,0:T(8,128)(2,1)S(1)}, bf16[32,2048]{1,0:T(8,128)(2,1)S(1)}, bf16[32,2048]{1,0:T(8,128)(2,1)S(1)}, bf16[32,2048]{1,0:T(8,128)(2,1)S(1)}, f32[1,2048]{1,0:T(1,128)S(1)}) custom-call(bf16[32,4096]{1,0:T(8,128)(2,1)S(1)} %copy-done.1, bf16[32,4096]{1,0:T(8,128)(2,1)S(1)} %collective-permute-done.refs_1_, ...), custom_call_target="tpu_custom_call" | custom-call | flops 1610612736 | bytes 12582912 | tf_op jit(solution)/shard_map/pallas_call | solution.py:416
  88.9 3.6 %shard_map.99 = (bf16[32,2048]{1,0:T(8,128)(2,1)S(1)}, bf16[32,2048]{1,0:T(8,128)(2,1)S(1)}, bf16[32,2048]{1,0:T(8,128)(2,1)S(1)}, bf16[32,2048]{1,0:T(8,128)(2,1)S(1)}, f32[1,2048]{1,0:T(1,128)S(1)}) custom-call(bf16[32,4096]{1,0:T(8,128)(2,1)S(1)} %copy-done.1, bf16[32,4096]{1,0:T(8,128)(2,1)S(1)} %collective-permute-done.refs_1_, ...), custom_call_target="tpu_custom_call" | custom-call | flops 1610612736 | bytes 12582912 | tf_op jit(solution)/shard_map/pallas_call | solution.py:416
  93.1 1.6 collective-permute-start.11
  95.7 3.8 %collective-permute-done.11.refs_5_ = bf16[32,2048]{1,0:T(8,128)(2,1)S(1)} collective-permute-done((bf16[32,2048]{1,0:T(8,128)(2,1)S(1)}, bf16[32,2048]{1,0:T(8,128)(2,1)S(1)}, u32[]{:S(2)}, u32[]{:S(2)}) %collective-permute-start.11) | collective-permute-done | bytes 131104 | tf_op jit(solution)/shard_map/ppermute | solution.py:206
  99.5 1.9 %collective-permute-done.8.refs_2_ = bf16[32,2048]{1,0:T(8,128)(2,1)S(1)} collective-permute-done((bf16[32,2048]{1,0:T(8,128)(2,1)S(1)}, bf16[32,2048]{1,0:T(8,128)(2,1)S(1)}, u32[]{:S(2)}, u32[]{:S(2)}) %collective-permute-start.8) | collective-permute-done | bytes 131104 | tf_op jit(solution)/shard_map/ppermute | solution.py:206
  101.8 1.6 collective-permute-start.13
  103.3 5.9 %collective-permute-done.13.refs_2_ = bf16[32,4096]{1,0:T(8,128)(2,1)S(1)} collective-permute-done((bf16[32,4096]{1,0:T(8,128)(2,1)S(1)}, bf16[32,4096]{1,0:T(8,128)(2,1)S(1)}, u32[]{:S(2)}, u32[]{:S(2)}) %collective-permute-start.13) | collective-permute-done | bytes 262176 | tf_op jit(solution)/shard_map/ppermute | solution.py:191
  109.3 1.5 collective-permute-done.14.refs_3_
  110.8 2.3 %shard_map.102 = bf16[8,1,1,128,128]{4,3,2,1,0:T(8,128)(2,1)S(1)} custom-call(bf16[32,4096]{1,0:T(8,128)(2,1)S(1)} %get-tuple-element.65.refs_0_, bf16[32,4096]{1,0:T(8,128)(2,1)S(1)} %collective-permute-done.12.refs_1_, bf16[32,4096]{1,0:T(8,128)(2,1)S(1)} %collective-permute-done.13.refs_2_, bf16[32,4096]{1,0:T(8,128)(2,1)S(1)} %collective-permute-done.14.refs_3_, ...), custom_call_target="tpu_custom_call" | custom-call | flops 1073741824 | bytes 8388608 | tf_op jit(solution)/shard_map/pallas_call | solution.py:306
  113.2 12.7 %all_to_all.22.g_ref = bf16[8,1,1,128,128]{4,3,2,1,0:T(8,128)(2,1)S(1)} all-to-all(bf16[8,1,1,128,128]{4,3,2,1,0:T(8,128)(2,1)S(1)} %shard_map.102), channel_id=1, replica_groups=mesh['seq'=8,'tensor'=4] {'seq'}, dimensions={0} | all-to-all | bytes 524288 | tf_op jit(solution)/shard_map/all_to_all | solution.py:228
  125.8 1.8 shard_map.103
  127.6 23.2 %all_to_all.23.refs_5_ = bf16[8,3,1,128,128]{4,3,2,1,0:T(8,128)(2,1)S(1)} all-to-all(bf16[8,3,1,128,128]{4,3,2,1,0:T(8,128)(2,1)S(1)} %shard_map.103), channel_id=1, replica_groups=mesh['seq'=8,'tensor'=4] {'seq'}, dimensions={0} | all-to-all | bytes 1572864 | tf_op jit(solution)/shard_map/all_to_all | solution.py:228
  150.8 3.6 %shard_map.105 = (bf16[32,2048]{1,0:T(8,128)(2,1)S(1)}, bf16[32,2048]{1,0:T(8,128)(2,1)S(1)}, bf16[32,2048]{1,0:T(8,128)(2,1)S(1)}, bf16[32,2048]{1,0:T(8,128)(2,1)S(1)}, f32[1,2048]{1,0:T(1,128)S(1)}) custom-call(bf16[32,4096]{1,0:T(8,128)(2,1)S(1)} %copy-done.1, bf16[32,4096]{1,0:T(8,128)(2,1)S(1)} %collective-permute-done.refs_1_, ...), custom_call_target="tpu_custom_call" | custom-call | flops 1610612736 | bytes 12582912 | tf_op jit(solution)/shard_map/pallas_call | solution.py:416
  154.3 3.6 %shard_map.104 = (bf16[32,2048]{1,0:T(8,128)(2,1)S(1)}, bf16[32,2048]{1,0:T(8,128)(2,1)S(1)}, bf16[32,2048]{1,0:T(8,128)(2,1)S(1)}, bf16[32,2048]{1,0:T(8,128)(2,1)S(1)}, f32[1,2048]{1,0:T(1,128)S(1)}) custom-call(bf16[32,4096]{1,0:T(8,128)(2,1)S(1)} %copy-done.1, bf16[32,4096]{1,0:T(8,128)(2,1)S(1)} %collective-permute-done.refs_1_, ...), custom_call_target="tpu_custom_call" | custom-call | flops 1610612736 | bytes 12582912 | tf_op jit(solution)/shard_map/pallas_call | solution.py:416
  158.0 1.2 collective-permute-done.21
  159.2 1.1 collective-permute-start.24
  160.3 1.4 collective-permute-start.23
  161.7 1.8 %collective-permute-start.22 = (f32[4096]{0:T(1024)S(1)}, f32[4096]{0:T(1024)S(1)}, u32[]{:S(2)}, u32[]{:S(2)}) collective-permute-start(f32[4096]{0:T(1024)S(1)} %add.49), channel_id=1, source_target_pairs={{0,8},{1,9},{2,10},{3,11},{4,12},{5,13},{6,14},{7,15},{8,0},{9,1},... | collective-permute-start | bytes 49160 | tf_op jit(solution)/shard_map/ppermute | solution.py:220
  165.5 2.4 %collective-permute-start.27 = (f32[4096]{0:T(1024)S(1)}, f32[4096]{0:T(1024)S(1)}, u32[]{:S(2)}, u32[]{:S(2)}) collective-permute-start(f32[4096]{0:T(1024)S(1)} %add_add_fusion), channel_id=1, source_target_pairs={{0,6},{1,7},{2,4},{3,5},{4,2},{5,3},{6,0},{7,1},{8,14},{9,15},{10,... | collective-permute-start | bytes 49160 | tf_op jit(solution)/shard_map/ppermute | solution.py:220
  169.2 1.0 collective-permute-done.27
  170.2 1.5 collective-permute-start.20
  173.2 3.0 %collective-permute-done.20.refs_5_ = bf16[32,2048]{1,0:T(8,128)(2,1)S(1)} collective-permute-done((bf16[32,2048]{1,0:T(8,128)(2,1)S(1)}, bf16[32,2048]{1,0:T(8,128)(2,1)S(1)}, u32[]{:S(2)}, u32[]{:S(2)}) %collective-permute-start.20) | collective-permute-done | bytes 131104 | tf_op jit(solution)/shard_map/ppermute | solution.py:206
  176.1 1.4 collective-permute-done.17.refs_2_
  177.5 1.2 shard_map.106
  (71 shorter events, 9.6 us)
Async XLA Ops:
  0.6 13.0 %collective-permute-start.4 = (bf16[32,4096]{1,0:T(8,128)(2,1)}, bf16[32,4096]{1,0:T(8,128)(2,1)S(1)}, u32[]{:S(2)}, u32[]{:S(2)}) collective-permute-start(bf16[32,4096]{1,0:T(8,128)(2,1)} %refs_9_.3), channel_id=1, source_target_pairs={{0,2},{1,3},{2,0},{3,1},{4,6},{5,7},{6,4},{7,5},{8,10},{9,11},{10,... | collective-permute-start | bytes 786440 | tf_op jit(solution)/shard_map/ppermute | solution.py:191
  3.7 12.3 %collective-permute-start.3 = (bf16[32,4096]{1,0:T(8,128)(2,1)}, bf16[32,4096]{1,0:T(8,128)(2,1)S(1)}, u32[]{:S(2)}, u32[]{:S(2)}) collective-permute-start(bf16[32,4096]{1,0:T(8,128)(2,1)} %refs_9_.3), channel_id=1, source_target_pairs={{0,1},{1,0},{2,3},{3,2},{4,5},{5,4},{6,7},{7,6},{8,9},{9,8},{10,11... | collective-permute-start | bytes 786440 | tf_op jit(solution)/shard_map/ppermute | solution.py:191
  3.7 12.1 %collective-permute-start.1 = (bf16[32,4096]{1,0:T(8,128)(2,1)}, bf16[32,4096]{1,0:T(8,128)(2,1)S(1)}, u32[]{:S(2)}, u32[]{:S(2)}) collective-permute-start(bf16[32,4096]{1,0:T(8,128)(2,1)} %refs_6_.3), channel_id=1, source_target_pairs={{0,2},{1,3},{2,0},{3,1},{4,6},{5,7},{6,4},{7,5},{8,10},{9,11},{10,... | collective-permute-start | bytes 786440 | tf_op jit(solution)/shard_map/ppermute | solution.py:191
  3.8 14.5 %collective-permute-start = (bf16[32,4096]{1,0:T(8,128)(2,1)}, bf16[32,4096]{1,0:T(8,128)(2,1)S(1)}, u32[]{:S(2)}, u32[]{:S(2)}) collective-permute-start(bf16[32,4096]{1,0:T(8,128)(2,1)} %refs_6_.3), channel_id=1, source_target_pairs={{0,1},{1,0},{2,3},{3,2},{4,5},{5,4},{6,7},{7,6},{8,9},{9,8},{10,11... | collective-permute-start | bytes 786440 | tf_op jit(solution)/shard_map/ppermute | solution.py:191
  4.2 11.8 %copy-start.2 = (bf16[32,4096]{1,0:T(8,128)(2,1)S(1)}, bf16[32,4096]{1,0:T(8,128)(2,1)}, u32[]{:S(2)}) copy-start(bf16[32,4096]{1,0:T(8,128)(2,1)} %refs_9_.3) | copy-start | bytes 786436
  13.6 2.4 %collective-permute-start.5 = (bf16[32,4096]{1,0:T(8,128)(2,1)S(1)}, bf16[32,4096]{1,0:T(8,128)(2,1)S(1)}, u32[]{:S(2)}, u32[]{:S(2)}) collective-permute-start(bf16[32,4096]{1,0:T(8,128)(2,1)S(1)} %collective-permute-done.4.refs_2_), channel_id=1, source_target_pairs={{0,1},{1,0},{2,3},{3,2},{4,5},{5,4},{6,7},{7,6},{8,9},{9,8},{10,11... | collective-permute-start | bytes 786440 | tf_op jit(solution)/shard_map/ppermute | solution.py:191
  15.8 2.6 %collective-permute-start.2 = (bf16[32,4096]{1,0:T(8,128)(2,1)S(1)}, bf16[32,4096]{1,0:T(8,128)(2,1)S(1)}, u32[]{:S(2)}, u32[]{:S(2)}) collective-permute-start(bf16[32,4096]{1,0:T(8,128)(2,1)S(1)} %collective-permute-done.1.refs_2_), channel_id=1, source_target_pairs={{0,1},{1,0},{2,3},{3,2},{4,5},{5,4},{6,7},{7,6},{8,9},{9,8},{10,11... | collective-permute-start | bytes 786440 | tf_op jit(solution)/shard_map/ppermute | solution.py:191
  18.4 37.4 %copy-start.4 = (s32[16,16]{1,0:T(8,128)S(1)}, s32[16,16]{1,0:T(8,128)}, u32[]{:S(2)}) copy-start(s32[16,16]{1,0:T(8,128)} %layout_ref.3) | copy-start | bytes 3076
  88.3 7.3 %collective-permute-start.9 = (bf16[32,2048]{1,0:T(8,128)(2,1)S(1)}, bf16[32,2048]{1,0:T(8,128)(2,1)S(1)}, u32[]{:S(2)}, u32[]{:S(2)}) collective-permute-start(bf16[32,2048]{1,0:T(8,128)(2,1)S(1)} %get-tuple-element.62), channel_id=1, source_target_pairs={{0,1},{1,0},{2,3},{3,2},{4,5},{5,4},{6,7},{7,6},{8,9},{9,8},{10,11... | collective-permute-start | bytes 393224 | tf_op jit(solution)/shard_map/ppermute | solution.py:206
  88.4 22.4 %slice-start = ((s8[8388608]{0:T(1024)(128)(4,1)}), s8[4194304]{0:T(1024)(128)(4,1)S(1)}, s32[]{:S(2)}) async-start(s8[8388608]{0:T(1024)(128)(4,1)} %bitcast.6), calls=%async_computation.4 | async-start | bytes 8388608
  88.4 22.4 %slice-start.1 = ((s8[8388608]{0:T(1024)(128)(4,1)}), s8[4194304]{0:T(1024)(128)(4,1)S(1)}, s32[]{:S(2)}) async-start(s8[8388608]{0:T(1024)(128)(4,1)} %bitcast.6), calls=%async_computation.5 | async-start | bytes 8388608
  88.4 4.6 %collective-permute-start.10 = (bf16[32,2048]{1,0:T(8,128)(2,1)S(1)}, bf16[32,2048]{1,0:T(8,128)(2,1)S(1)}, u32[]{:S(2)}, u32[]{:S(2)}) collective-permute-start(bf16[32,2048]{1,0:T(8,128)(2,1)S(1)} %get-tuple-element.64), channel_id=1, source_target_pairs={{0,1},{1,0},{2,3},{3,2},{4,5},{5,4},{6,7},{7,6},{8,9},{9,8},{10,11... | collective-permute-start | bytes 393224 | tf_op jit(solution)/shard_map/ppermute | solution.py:206
  92.5 3.2 %collective-permute-start.6 = (bf16[32,2048]{1,0:T(8,128)(2,1)S(1)}, bf16[32,2048]{1,0:T(8,128)(2,1)S(1)}, u32[]{:S(2)}, u32[]{:S(2)}) collective-permute-start(bf16[32,2048]{1,0:T(8,128)(2,1)S(1)} %get-tuple-element.58), channel_id=1, source_target_pairs={{0,1},{1,0},{2,3},{3,2},{4,5},{5,4},{6,7},{7,6},{8,9},{9,8},{10,11... | collective-permute-start | bytes 393224 | tf_op jit(solution)/shard_map/ppermute | solution.py:206
  92.6 2.0 %collective-permute-start.7 = (bf16[32,2048]{1,0:T(8,128)(2,1)S(1)}, bf16[32,2048]{1,0:T(8,128)(2,1)S(1)}, u32[]{:S(2)}, u32[]{:S(2)}) collective-permute-start(bf16[32,2048]{1,0:T(8,128)(2,1)S(1)} %get-tuple-element.60), channel_id=1, source_target_pairs={{0,1},{1,0},{2,3},{3,2},{4,5},{5,4},{6,7},{7,6},{8,9},{9,8},{10,11... | collective-permute-start | bytes 393224 | tf_op jit(solution)/shard_map/ppermute | solution.py:206
  93.1 6.4 %collective-permute-start.11 = (bf16[32,2048]{1,0:T(8,128)(2,1)S(1)}, bf16[32,2048]{1,0:T(8,128)(2,1)S(1)}, u32[]{:S(2)}, u32[]{:S(2)}) collective-permute-start(bf16[32,2048]{1,0:T(8,128)(2,1)S(1)} %add_convert_fusion.2), channel_id=1, source_target_pairs={{0,2},{1,3},{2,0},{3,1},{4,6},{5,7},{6,4},{7,5},{8,10},{9,11},{10,... | collective-permute-start | bytes 393224 | tf_op jit(solution)/shard_map/ppermute | solution.py:206
  94.7 6.8 %collective-permute-start.8 = (bf16[32,2048]{1,0:T(8,128)(2,1)S(1)}, bf16[32,2048]{1,0:T(8,128)(2,1)S(1)}, u32[]{:S(2)}, u32[]{:S(2)}) collective-permute-start(bf16[32,2048]{1,0:T(8,128)(2,1)S(1)} %add_convert_fusion.3), channel_id=1, source_target_pairs={{0,2},{1,3},{2,0},{3,1},{4,6},{5,7},{6,4},{7,5},{8,10},{9,11},{10,... | collective-permute-start | bytes 393224 | tf_op jit(solution)/shard_map/ppermute | solution.py:206
  101.8 7.5 %collective-permute-start.13 = (bf16[32,4096]{1,0:T(8,128)(2,1)S(1)}, bf16[32,4096]{1,0:T(8,128)(2,1)S(1)}, u32[]{:S(2)}, u32[]{:S(2)}) collective-permute-start(bf16[32,4096]{1,0:T(8,128)(2,1)S(1)} %get-tuple-element.65.refs_0_), channel_id=1, source_target_pairs={{0,2},{1,3},{2,0},{3,1},{4,6},{5,7},{6,4},{7,5},{8,10},{9,11},{10,... | collective-permute-start | bytes 786440 | tf_op jit(solution)/shard_map/ppermute | solution.py:191
  103.3 6.0 %collective-permute-start.12 = (bf16[32,4096]{1,0:T(8,128)(2,1)S(1)}, bf16[32,4096]{1,0:T(8,128)(2,1)S(1)}, u32[]{:S(2)}, u32[]{:S(2)}) collective-permute-start(bf16[32,4096]{1,0:T(8,128)(2,1)S(1)} %get-tuple-element.65.refs_0_), channel_id=1, source_target_pairs={{0,1},{1,0},{2,3},{3,2},{4,5},{5,4},{6,7},{7,6},{8,9},{9,8},{10,11... | collective-permute-start | bytes 786440 | tf_op jit(solution)/shard_map/ppermute | solution.py:191
  109.3 1.5 collective-permute-start.14
  157.9 1.2 collective-permute-start.21
  159.2 5.5 %collective-permute-start.24 = (f32[4096]{0:T(1024)S(1)}, f32[4096]{0:T(1024)S(1)}, u32[]{:S(2)}, u32[]{:S(2)}) collective-permute-start(f32[4096]{0:T(1024)S(1)} %add.49), channel_id=1, source_target_pairs={{0,24},{1,25},{2,26},{3,27},{4,28},{5,29},{6,30},{7,31},{8,16},{9,... | collective-permute-start | bytes 49160 | tf_op jit(solution)/shard_map/ppermute | solution.py:220
  160.3 4.8 %collective-permute-start.23 = (f32[4096]{0:T(1024)S(1)}, f32[4096]{0:T(1024)S(1)}, u32[]{:S(2)}, u32[]{:S(2)}) collective-permute-start(f32[4096]{0:T(1024)S(1)} %add.49), channel_id=1, source_target_pairs={{0,16},{1,17},{2,18},{3,19},{4,20},{5,21},{6,22},{7,23},{8,24},{9,... | collective-permute-start | bytes 49160 | tf_op jit(solution)/shard_map/ppermute | solution.py:220
  161.7 3.7 %collective-permute-start.22 = (f32[4096]{0:T(1024)S(1)}, f32[4096]{0:T(1024)S(1)}, u32[]{:S(2)}, u32[]{:S(2)}) collective-permute-start(f32[4096]{0:T(1024)S(1)} %add.49), channel_id=1, source_target_pairs={{0,8},{1,9},{2,10},{3,11},{4,12},{5,13},{6,14},{7,15},{8,0},{9,1},... | collective-permute-start | bytes 49160 | tf_op jit(solution)/shard_map/ppermute | solution.py:220
  163.6 9.6 %collective-permute-start.18 = (bf16[32,2048]{1,0:T(8,128)(2,1)S(1)}, bf16[32,2048]{1,0:T(8,128)(2,1)S(1)}, u32[]{:S(2)}, u32[]{:S(2)}) collective-permute-start(bf16[32,2048]{1,0:T(8,128)(2,1)S(1)} %get-tuple-element.73), channel_id=1, source_target_pairs={{0,1},{1,0},{2,3},{3,2},{4,5},{5,4},{6,7},{7,6},{8,9},{9,8},{10,11... | collective-permute-start | bytes 393224 | tf_op jit(solution)/shard_map/ppermute | solution.py:206
  163.6 4.3 %collective-permute-start.19 = (bf16[32,2048]{1,0:T(8,128)(2,1)S(1)}, bf16[32,2048]{1,0:T(8,128)(2,1)S(1)}, u32[]{:S(2)}, u32[]{:S(2)}) collective-permute-start(bf16[32,2048]{1,0:T(8,128)(2,1)S(1)} %get-tuple-element.75), channel_id=1, source_target_pairs={{0,1},{1,0},{2,3},{3,2},{4,5},{5,4},{6,7},{7,6},{8,9},{9,8},{10,11... | collective-permute-start | bytes 393224 | tf_op jit(solution)/shard_map/ppermute | solution.py:206
  164.7 8.4 %collective-permute-start.15 = (bf16[32,2048]{1,0:T(8,128)(2,1)S(1)}, bf16[32,2048]{1,0:T(8,128)(2,1)S(1)}, u32[]{:S(2)}, u32[]{:S(2)}) collective-permute-start(bf16[32,2048]{1,0:T(8,128)(2,1)S(1)} %get-tuple-element.69), channel_id=1, source_target_pairs={{0,1},{1,0},{2,3},{3,2},{4,5},{5,4},{6,7},{7,6},{8,9},{9,8},{10,11... | collective-permute-start | bytes 393224 | tf_op jit(solution)/shard_map/ppermute | solution.py:206
  165.1 3.5 %collective-permute-start.16 = (bf16[32,2048]{1,0:T(8,128)(2,1)S(1)}, bf16[32,2048]{1,0:T(8,128)(2,1)S(1)}, u32[]{:S(2)}, u32[]{:S(2)}) collective-permute-start(bf16[32,2048]{1,0:T(8,128)(2,1)S(1)} %get-tuple-element.71), channel_id=1, source_target_pairs={{0,1},{1,0},{2,3},{3,2},{4,5},{5,4},{6,7},{7,6},{8,9},{9,8},{10,11... | collective-permute-start | bytes 393224 | tf_op jit(solution)/shard_map/ppermute | solution.py:206
  165.5 4.7 %collective-permute-start.27 = (f32[4096]{0:T(1024)S(1)}, f32[4096]{0:T(1024)S(1)}, u32[]{:S(2)}, u32[]{:S(2)}) collective-permute-start(f32[4096]{0:T(1024)S(1)} %add_add_fusion), channel_id=1, source_target_pairs={{0,6},{1,7},{2,4},{3,5},{4,2},{5,3},{6,0},{7,1},{8,14},{9,15},{10,... | collective-permute-start | bytes 49160 | tf_op jit(solution)/shard_map/ppermute | solution.py:220
  167.9 3.8 %collective-permute-start.26 = (f32[4096]{0:T(1024)S(1)}, f32[4096]{0:T(1024)S(1)}, u32[]{:S(2)}, u32[]{:S(2)}) collective-permute-start(f32[4096]{0:T(1024)S(1)} %add_add_fusion), channel_id=1, source_target_pairs={{0,4},{1,5},{2,6},{3,7},{4,0},{5,1},{6,2},{7,3},{8,12},{9,13},{10,... | collective-permute-start | bytes 49160 | tf_op jit(solution)/shard_map/ppermute | solution.py:220
  168.6 4.0 %collective-permute-start.25 = (f32[4096]{0:T(1024)S(1)}, f32[4096]{0:T(1024)S(1)}, u32[]{:S(2)}, u32[]{:S(2)}) collective-permute-start(f32[4096]{0:T(1024)S(1)} %add_add_fusion), channel_id=1, source_target_pairs={{0,2},{1,3},{2,0},{3,1},{4,6},{5,7},{6,4},{7,5},{8,10},{9,11},{10,... | collective-permute-start | bytes 49160 | tf_op jit(solution)/shard_map/ppermute | solution.py:220
  170.2 5.9 %collective-permute-start.20 = (bf16[32,2048]{1,0:T(8,128)(2,1)S(1)}, bf16[32,2048]{1,0:T(8,128)(2,1)S(1)}, u32[]{:S(2)}, u32[]{:S(2)}) collective-permute-start(bf16[32,2048]{1,0:T(8,128)(2,1)S(1)} %add_convert_fusion), channel_id=1, source_target_pairs={{0,2},{1,3},{2,0},{3,1},{4,6},{5,7},{6,4},{7,5},{8,10},{9,11},{10,... | collective-permute-start | bytes 393224 | tf_op jit(solution)/shard_map/ppermute | solution.py:206
  171.7 5.8 %collective-permute-start.17 = (bf16[32,2048]{1,0:T(8,128)(2,1)S(1)}, bf16[32,2048]{1,0:T(8,128)(2,1)S(1)}, u32[]{:S(2)}, u32[]{:S(2)}) collective-permute-start(bf16[32,2048]{1,0:T(8,128)(2,1)S(1)} %add_convert_fusion.1), channel_id=1, source_target_pairs={{0,2},{1,3},{2,0},{3,1},{4,6},{5,7},{6,4},{7,5},{8,10},{9,11},{10,... | collective-permute-start | bytes 393224 | tf_op jit(solution)/shard_map/ppermute | solution.py:206
  (3 other events, 22.3 us)
